TPU v7x, 32 devices: a whole 2x2x4 slice. The times are simulated.
32 devices in a mesh: gx: 4 (over z), gy: 4 (over x, core), gz: 2 (over y).
Axes of the slice: x: 2, y: 2, z: 4, core: 2. Of those that a mesh axis runs over, the one named last changes fastest.
Arguments:
- charges: bfloat16 [256, 256, 256], P('gx', 'gy', 'gz'), may hold values from -6 to 6
- taps: float32 [4, 4, 17], replicated, may hold values from 0.05 to 0.3
Outputs:
- potential: bfloat16 [256, 256, 256], P('gx', 'gy', 'gz')
All inputs are finite; a program needn't handle non-finite values.
Results may differ from a plain program's by a relative error of at most 0.012.
The roundings to bfloat16 on the way count: a program that leaves them out, or rounds other values in their place, can miss the bound.
Values may be sent and summed in bfloat16 or wider, within the bound.
No kernel may reach another device: no remote copies, remote signals or barrier semaphores. Data moves between devices by JAX's collectives and lax.ppermute only.
A program may use at most 128 MiB of HBM per device.

v0:
```python
import jax
import jax.numpy as jnp
from jax import lax
from jax.sharding import PartitionSpec as P


def padded_2(value, sides, width):
    for axis, dim in sides:
        count, length = (lax.axis_size(axis), value.shape[dim])
        up = [(i, (i + 1) % count) for i in range(count)]
        down = [(j, i) for i, j in up]
        last = lax.slice_in_dim(value, length - width, length, axis=dim)
        first = lax.slice_in_dim(value, 0, width, axis=dim)
        before = lax.ppermute(last, axis, up)
        after = lax.ppermute(first, axis, down)
        value = jnp.concatenate([before, value, after], axis=dim)
    return value


def restrict_padded(padded):
    for along in range(3):
        fine_count = padded.shape[along] - 6

        def strided(offset):
            return lax.slice_in_dim(padded, 3 + offset, 3 + offset + fine_count, 2, along)

        padded = (
            16.0 * strided(0) + 9.0 * (strided(-1) + strided(1)) - (strided(-3) + strided(3))
        ) / 16.0
    return padded


def prolong_padded(padded):
    for along in range(3):
        coarse_count = padded.shape[along] - 4

        def shifted(start):
            return lax.slice_in_dim(padded, start, start + coarse_count, 1, along)

        centre = shifted(2)
        between = (9.0 * (centre + shifted(3)) - (shifted(1) + shifted(4))) / 16.0
        shape_list = list(centre.shape)
        shape_list[along] = 2 * coarse_count
        padded = jnp.stack([centre, between], along + 1).reshape(shape_list)
    return padded


def widen(field, width):
    return padded_2(field, (("gx", 0), ("gy", 1), ("gz", 2)), width)


def band(tap_row, length):
    row_ids = lax.broadcasted_iota(jnp.int32, (length + 16, length), 0)
    col_ids = lax.broadcasted_iota(jnp.int32, (length + 16, length), 1)
    offsets = row_ids - col_ids
    matrix = jnp.zeros((length + 16, length), jnp.float32)
    for offset in range(tap_row.shape[0]):
        matrix = jnp.where(offsets == offset, tap_row[offset].astype(jnp.float32), matrix)
    return matrix.astype(jnp.bfloat16)


def pick_tile(length):
    if length <= 64:
        return length
    for candidate in (64, 56, 48, 46, 40, 32, 24, 23, 16):
        return candidate
    return length


def pass_along(padded, tap_row, along, length):
    rank_count = padded.ndim
    letters = "abcdefg"[:rank_count]
    tile_len = pick_tile(length)
    if tile_len == length:
        matrix = band(tap_row, length)
        target = letters[:along] + "w" + letters[along + 1 :]
        return jnp.einsum(
            letters + "," + letters[along] + "w->" + target,
            padded,
            matrix,
            preferred_element_type=jnp.float32,
        )
    tile_count = length // tile_len
    matrix = band(tap_row, tile_len)
    widths = [(0, 0)] * rank_count
    widths[along] = (0, tile_len - 16)
    filled = jnp.pad(padded, widths)
    shape_list = list(padded.shape)
    shape_list[along : along + 1] = [tile_count + 1, tile_len]
    tiled = filled.reshape(shape_list)
    leading = lax.slice_in_dim(tiled, 0, tile_count, 1, along)
    trailing = lax.slice_in_dim(
        lax.slice_in_dim(tiled, 1, tile_count + 1, 1, along), 0, 16, 1, along + 1
    )
    source = letters[:along] + "pq" + letters[along + 1 :]
    target = letters[:along] + "pr" + letters[along + 1 :]
    result = jnp.einsum(
        source + ",qr->" + target, leading, matrix[:tile_len], preferred_element_type=jnp.float32
    )
    result = result + jnp.einsum(
        source + ",qr->" + target, trailing, matrix[tile_len:], preferred_element_type=jnp.float32
    )
    out_shape = list(padded.shape)
    out_shape[along] = length
    return result.reshape(out_shape)


def convolve(padded, level_taps, out_x, out_y, out_z):
    potential = jnp.zeros((out_x, out_y, out_z), jnp.float32)
    for term in range(level_taps.shape[0]):
        section = pass_along(padded, level_taps[term], 2, out_z).astype(jnp.bfloat16)
        section = pass_along(section, level_taps[term], 1, out_y).astype(jnp.bfloat16)
        potential = potential + pass_along(section, level_taps[term], 0, out_x)
    return potential


def kernel_local(field, level_taps):
    charged = field.astype(jnp.bfloat16)
    padded = padded_2(charged, (("gx", 0), ("gy", 1), ("gz", 2)), 8)
    potential = convolve(padded, level_taps, field.shape[0], field.shape[1], field.shape[2])
    return potential


def per_device(charges, taps):
    level_taps = taps.astype(jnp.bfloat16)
    level_zero = charges.astype(jnp.float32)
    level_one = restrict_padded(widen(level_zero, 3))
    level_two = restrict_padded(widen(level_one, 3))
    level_three = restrict_padded(widen(level_two, 3))
    kernel_zero = kernel_local(level_zero, level_taps[0])
    kernel_one = kernel_local(level_one, level_taps[1])
    kernel_two = kernel_local(level_two, level_taps[2])
    block_x, block_y, block_z = level_three.shape
    count_x = lax.axis_size("gx")
    count_y = lax.axis_size("gy")
    count_z = lax.axis_size("gz")
    pieces = lax.all_gather(
        level_three.astype(jnp.bfloat16).reshape(1, block_x * block_y * block_z),
        ("gx", "gy", "gz"),
        axis=0,
        tiled=True,
    )
    top_grid = pieces.reshape(count_x, count_y, count_z, block_x, block_y, block_z).transpose(
        0, 3, 1, 4, 2, 5
    )
    top_grid = top_grid.reshape(count_x * block_x, count_y * block_y, count_z * block_z)
    corner = (
        lax.axis_index("gx") * block_x,
        lax.axis_index("gy") * block_y,
        lax.axis_index("gz") * block_z,
    )
    charge_window = lax.dynamic_slice(
        jnp.pad(top_grid, 10, mode="wrap"), corner, (block_x + 20, block_y + 20, block_z + 20)
    )
    window = convolve(charge_window, level_taps[3], block_x + 4, block_y + 4, block_z + 4)
    potential_two = kernel_two + prolong_padded(window)
    potential_one = kernel_one + prolong_padded(widen(potential_two, 2))
    potential_zero = kernel_zero + prolong_padded(widen(potential_one, 2))
    return potential_zero.astype(jnp.bfloat16)


def solution(mesh):
    return jax.shard_map(
        per_device,
        mesh=mesh,
        in_specs=(P("gx", "gy", "gz"), P()),
        out_specs=P("gx", "gy", "gz"),
        check_vma=False,
    )
```

profile of v0, /device:TPU:0, one launch (start us, length us, event | category | flops | bytes accessed | tf_op | source)
XLA Modules:
  0.0 814.1 jit_solution(8965799550738029879)
XLA Ops:
  31.0 11.3 %select_convert_fusion.5 = bf16[80,64]{0,1:T(8,128)(2,1)} fusion(bf16[]{:T(256)} %bitcast.617, bf16[]{:T(256)} %bitcast.616, bf16[]{:T(256)} %bitcast.615, bf16[]{:T(256)} %bitcast.614, bf16[]{:T(256)} %bitcast.613, bf16[]{:T(256)} %bitcast.612, bf16[]{:T(256)} %bitcast.611, bf16[]{:T(256)} %bitcast.610, bf16[]{:T(256)} %bitcast.609, bf16[]{:T(256)} %bitcast.608, ...), kind=kLoop, calls=%fused_computation.239 | loop fusion | flops 179200 | bytes 10274 | tf_op jit(solution)/shard_map/convert_element_type | solution.py:59
  42.3 11.8 %select_convert_fusion.6 = bf16[80,64]{0,1:T(8,128)(2,1)} fusion(bf16[]{:T(256)} %bitcast.599, bf16[]{:T(256)} %bitcast.598, bf16[]{:T(256)} %bitcast.597, bf16[]{:T(256)} %bitcast.596, bf16[]{:T(256)} %bitcast.595, bf16[]{:T(256)} %bitcast.594, bf16[]{:T(256)} %bitcast.593, bf16[]{:T(256)} %bitcast.592, bf16[]{:T(256)} %bitcast.591, bf16[]{:T(256)} %bitcast.590, ...), kind=kLoop, calls=%fused_computation.240 | loop fusion | flops 179200 | bytes 10274 | tf_op jit(solution)/shard_map/convert_element_type | solution.py:59
  54.1 11.3 %select_convert_fusion.7 = bf16[80,64]{0,1:T(8,128)(2,1)} fusion(bf16[]{:T(256)} %bitcast.581, bf16[]{:T(256)} %bitcast.580, bf16[]{:T(256)} %bitcast.579, bf16[]{:T(256)} %bitcast.578, bf16[]{:T(256)} %bitcast.577, bf16[]{:T(256)} %bitcast.576, bf16[]{:T(256)} %bitcast.575, bf16[]{:T(256)} %bitcast.574, bf16[]{:T(256)} %bitcast.573, bf16[]{:T(256)} %bitcast.572, ...), kind=kLoop, calls=%fused_computation.241 | loop fusion | flops 179200 | bytes 10274 | tf_op jit(solution)/shard_map/convert_element_type | solution.py:59
  249.1 68.6 %all-gather = bf16[32,1,1024]{2,1,0:T(2,128)(2,1)S(1)} all-gather(bf16[1,1,1024]{2,1,0:T(2,128)(2,1)S(1)} %reshape.1455), channel_id=1, replica_groups=mesh['gx'=4,'gy'=4,'gz'=2] {'gx','gy','gz'}, dimensions={0}, use_global_device_ids=true | all-gather | bytes 67584 | tf_op jit(solution)/shard_map/all_gather | solution.py:137
  322.4 11.1 %convolution_convert_fusion.13 = bf16[28,28,20]{1,2,0:T(8,128)(2,1)S(1)} fusion(bf16[28,28,36]{2,1,0:T(8,128)(2,1)S(1)} %fusion.79, bf16[]{:T(256)} %bitcast.498, bf16[]{:T(256)} %bitcast.497, bf16[]{:T(256)} %bitcast.496, bf16[]{:T(256)} %bitcast.495, bf16[]{:T(256)} %bitcast.494, bf16[]{:T(256)} %bitcast.493, bf16[]{:T(256)} %bitcast.492, bf16[]{:T(256)} %bitcast.491, ...), kind=kOutput, calls=%fused_computation.72 | convolution fusion | flops 1169840 | bytes 87842 | tf_op jit(solution)/shard_map/abc,cw->abw/dot_general | solution.py:77
  333.5 11.0 %fusion.51 = bf16[28,12,20]{0,1,2:T(8,128)(2,1)S(1)} fusion(bf16[28,28,20]{1,2,0:T(8,128)(2,1)S(1)} %convolution_convert_fusion.13, bf16[]{:T(256)} %bitcast.498, bf16[]{:T(256)} %bitcast.497, bf16[]{:T(256)} %bitcast.496, bf16[]{:T(256)} %bitcast.495, bf16[]{:T(256)} %bitcast.494, bf16[]{:T(256)} %bitcast.493, bf16[]{:T(256)} %bitcast.492, bf16[]{:T(256)} %bitcast.491, ...), kind=kOutput, calls=%fused_computation.96 | convolution fusion | flops 394800 | bytes 44834 | tf_op jit(solution)/shard_map/abc,bw->awc/dot_general | solution.py:77
  344.5 11.0 %convolution_convert_fusion.14 = bf16[28,28,20]{1,2,0:T(8,128)(2,1)S(1)} fusion(bf16[28,28,36]{2,1,0:T(8,128)(2,1)S(1)} %fusion.79, bf16[]{:T(256)} %bitcast.461, bf16[]{:T(256)} %bitcast.460, bf16[]{:T(256)} %bitcast.459, bf16[]{:T(256)} %bitcast.458, bf16[]{:T(256)} %bitcast.457, bf16[]{:T(256)} %bitcast.456, bf16[]{:T(256)} %bitcast.455, bf16[]{:T(256)} %bitcast.454, ...), kind=kOutput, calls=%fused_computation.73 | convolution fusion | flops 1169840 | bytes 87842 | tf_op jit(solution)/shard_map/abc,cw->abw/dot_general | solution.py:77
  355.5 10.9 %fusion.50 = bf16[28,12,20]{0,1,2:T(8,128)(2,1)S(1)} fusion(bf16[28,28,20]{1,2,0:T(8,128)(2,1)S(1)} %convolution_convert_fusion.14, bf16[]{:T(256)} %bitcast.461, bf16[]{:T(256)} %bitcast.460, bf16[]{:T(256)} %bitcast.459, bf16[]{:T(256)} %bitcast.458, bf16[]{:T(256)} %bitcast.457, bf16[]{:T(256)} %bitcast.456, bf16[]{:T(256)} %bitcast.455, bf16[]{:T(256)} %bitcast.454, ...), kind=kOutput, calls=%fused_computation.95 | convolution fusion | flops 394800 | bytes 44834 | tf_op jit(solution)/shard_map/abc,bw->awc/dot_general | solution.py:77
  419.7 10.8 %convolution_add_fusion.8 = f32[12,12,20]{2,0,1:T(8,128)S(1)} fusion(f32[12,12,20]{2,0,1:T(8,128)S(1)} %fusion.104, bf16[28,12,20]{0,1,2:T(8,128)(2,1)S(1)} %fusion.50, bf16[]{:T(256)} %bitcast.461, bf16[]{:T(256)} %bitcast.460, bf16[]{:T(256)} %bitcast.459, bf16[]{:T(256)} %bitcast.458, bf16[]{:T(256)} %bitcast.457, bf16[]{:T(256)} %bitcast.456, ...), kind=kOutput, calls=%fused_computation.93 | convolution fusion | flops 175920 | bytes 36514 | tf_op jit(solution)/shard_map/abc,aw->wbc/dot_general | solution.py:77
  430.5 10.9 %convolution_add_fusion.7 = f32[12,12,20]{2,0,1:T(8,128)S(1)} fusion(f32[12,12,20]{2,0,1:T(8,128)S(1)} %convolution_add_fusion.8, bf16[28,12,20]{0,1,2:T(8,128)(2,1)S(1)} %fusion.51, bf16[]{:T(256)} %bitcast.498, bf16[]{:T(256)} %bitcast.497, bf16[]{:T(256)} %bitcast.496, bf16[]{:T(256)} %bitcast.495, bf16[]{:T(256)} %bitcast.494, bf16[]{:T(256)} %bitcast.493, ...), kind=kOutput, calls=%fused_computation.92 | convolution fusion | flops 175920 | bytes 36514 | tf_op jit(solution)/shard_map/abc,aw->wbc/dot_general | solution.py:77
  474.6 12.8 %fusion.14 = bf16[80,64,128]{2,1,0:T(8,128)(2,1)} fusion(bf16[80,80,128]{1,2,0:T(8,128)(2,1)S(1)} %bitcast.801, bf16[]{:T(256)} %bitcast.617, bf16[]{:T(256)} %bitcast.616, bf16[]{:T(256)} %bitcast.615, bf16[]{:T(256)} %bitcast.614, bf16[]{:T(256)} %bitcast.613, bf16[]{:T(256)} %bitcast.612, bf16[]{:T(256)} %bitcast.611, bf16[]{:T(256)} %bitcast.610, ...), kind=kOutput, calls=%fused_computation.33 | convolution fusion | flops 105692160 | bytes 2949154 | tf_op jit(solution)/shard_map/abc,bw->awc/dot_general | solution.py:77
  489.2 13.3 %fusion.13 = bf16[80,64,128]{2,1,0:T(8,128)(2,1)} fusion(bf16[80,80,128]{1,2,0:T(8,128)(2,1)S(1)} %bitcast.802, bf16[]{:T(256)} %bitcast.599, bf16[]{:T(256)} %bitcast.598, bf16[]{:T(256)} %bitcast.597, bf16[]{:T(256)} %bitcast.596, bf16[]{:T(256)} %bitcast.595, bf16[]{:T(256)} %bitcast.594, bf16[]{:T(256)} %bitcast.593, bf16[]{:T(256)} %bitcast.592, ...), kind=kOutput, calls=%fused_computation.32 | convolution fusion | flops 105692160 | bytes 2949154 | tf_op jit(solution)/shard_map/abc,bw->awc/dot_general | solution.py:77
  505.9 12.8 %fusion.12 = bf16[80,64,128]{2,1,0:T(8,128)(2,1)} fusion(bf16[80,80,128]{1,2,0:T(8,128)(2,1)S(1)} %bitcast.800, bf16[]{:T(256)} %bitcast.581, bf16[]{:T(256)} %bitcast.580, bf16[]{:T(256)} %bitcast.579, bf16[]{:T(256)} %bitcast.578, bf16[]{:T(256)} %bitcast.577, bf16[]{:T(256)} %bitcast.576, bf16[]{:T(256)} %bitcast.575, bf16[]{:T(256)} %bitcast.574, ...), kind=kOutput, calls=%fused_computation.31 | convolution fusion | flops 105692160 | bytes 2949154 | tf_op jit(solution)/shard_map/abc,bw->awc/dot_general | solution.py:77
  541.2 11.6 %fusion.45 = bf16[32,16,32]{2,1,0:T(8,128)(2,1)} fusion(bf16[32,32,48]{2,1,0:T(8,128)(2,1)S(1)} %pad_maximum_fusion.21, bf16[]{:T(256)} %bitcast.312, bf16[]{:T(256)} %bitcast.311, bf16[]{:T(256)} %bitcast.310, bf16[]{:T(256)} %bitcast.309, bf16[]{:T(256)} %bitcast.308, bf16[]{:T(256)} %bitcast.307, bf16[]{:T(256)} %bitcast.306, bf16[]{:T(256)} %bitcast.305, ...), kind=kOutput, calls=%fused_computation.80 | convolution fusion | flops 4315136 | bytes 131106 | tf_op jit(solution)/shard_map/abc,bw->awc/dot_general | solution.py:77
  552.9 11.6 %convolution_add_fusion.5 = f32[16,16,32]{2,0,1:T(8,128)S(1)} fusion(f32[16,16,32]{2,0,1:T(8,128)S(1)} %fusion.99, bf16[32,16,32]{2,1,0:T(8,128)(2,1)} %fusion.45, bf16[]{:T(256)} %bitcast.312, bf16[]{:T(256)} %bitcast.311, bf16[]{:T(256)} %bitcast.310, bf16[]{:T(256)} %bitcast.309, bf16[]{:T(256)} %bitcast.308, bf16[]{:T(256)} %bitcast.307, ...), kind=kOutput, calls=%fused_computation.85 | convolution fusion | flops 550400 | bytes 98338 | tf_op jit(solution)/shard_map/abc,aw->wbc/dot_general | solution.py:77
  564.5 11.6 %fusion.46 = bf16[32,16,32]{2,1,0:T(8,128)(2,1)} fusion(bf16[32,32,48]{2,1,0:T(8,128)(2,1)S(1)} %pad_maximum_fusion.21, bf16[]{:T(256)} %bitcast.349, bf16[]{:T(256)} %bitcast.348, bf16[]{:T(256)} %bitcast.347, bf16[]{:T(256)} %bitcast.346, bf16[]{:T(256)} %bitcast.345, bf16[]{:T(256)} %bitcast.344, bf16[]{:T(256)} %bitcast.343, bf16[]{:T(256)} %bitcast.342, ...), kind=kOutput, calls=%fused_computation.81 | convolution fusion | flops 4315136 | bytes 131106 | tf_op jit(solution)/shard_map/abc,bw->awc/dot_general | solution.py:77
  576.0 11.6 %convolution_add_fusion.4 = f32[16,16,32]{2,0,1:T(8,128)S(1)} fusion(f32[16,16,32]{2,0,1:T(8,128)S(1)} %convolution_add_fusion.5, bf16[32,16,32]{2,1,0:T(8,128)(2,1)} %fusion.46, bf16[]{:T(256)} %bitcast.349, bf16[]{:T(256)} %bitcast.348, bf16[]{:T(256)} %bitcast.347, bf16[]{:T(256)} %bitcast.346, bf16[]{:T(256)} %bitcast.345, bf16[]{:T(256)} %bitcast.344, ...), kind=kOutput, calls=%fused_computation.84 | convolution fusion | flops 550400 | bytes 98338 | tf_op jit(solution)/shard_map/abc,aw->wbc/dot_general | solution.py:77
  587.6 11.7 %fusion.47 = bf16[32,16,32]{2,1,0:T(8,128)(2,1)} fusion(bf16[32,32,48]{2,1,0:T(8,128)(2,1)S(1)} %pad_maximum_fusion.21, bf16[]{:T(256)} %bitcast.386, bf16[]{:T(256)} %bitcast.385, bf16[]{:T(256)} %bitcast.384, bf16[]{:T(256)} %bitcast.383, bf16[]{:T(256)} %bitcast.382, bf16[]{:T(256)} %bitcast.381, bf16[]{:T(256)} %bitcast.380, bf16[]{:T(256)} %bitcast.379, ...), kind=kOutput, calls=%fused_computation.82 | convolution fusion | flops 4315136 | bytes 131106 | tf_op jit(solution)/shard_map/abc,bw->awc/dot_general | solution.py:77
  599.3 11.7 %fusion.48 = f32[16,16,32]{2,0,1:T(8,128)S(1)} fusion(f32[16,16,32]{2,0,1:T(8,128)S(1)} %copy-done.17, f32[16,16,32]{2,0,1:T(8,128)S(1)} %convolution_add_fusion.4, bf16[32,16,32]{2,1,0:T(8,128)(2,1)} %fusion.47, bf16[]{:T(256)} %bitcast.386, bf16[]{:T(256)} %bitcast.385, bf16[]{:T(256)} %bitcast.384, bf16[]{:T(256)} %bitcast.383, bf16[]{:T(256)} %bitcast.382, ...), kind=kOutput, calls=%fused_computation.86 | convolution fusion | flops 558592 | bytes 131106 | tf_op jit(solution)/shard_map/abc,aw->wbc/dot_general | solution.py:77
  615.0 12.6 %fusion.15 = bf16[80,64,128]{2,1,0:T(8,128)(2,1)} fusion(bf16[80,80,128]{1,2,0:T(8,128)(2,1)S(1)} %bitcast.799, bf16[]{:T(256)} %bitcast.635, bf16[]{:T(256)} %bitcast.634, bf16[]{:T(256)} %bitcast.633, bf16[]{:T(256)} %bitcast.632, bf16[]{:T(256)} %bitcast.631, bf16[]{:T(256)} %bitcast.630, bf16[]{:T(256)} %bitcast.629, bf16[]{:T(256)} %bitcast.628, ...), kind=kOutput, calls=%fused_computation.34 | convolution fusion | flops 105692160 | bytes 2949154 | tf_op jit(solution)/shard_map/abc,bw->awc/dot_general | solution.py:77
  632.5 11.2 %fusion.35 = bf16[48,32,64]{2,1,0:T(8,128)(2,1)S(1)} fusion(bf16[48,48,80]{2,1,0:T(8,128)(2,1)S(1)} %pad_maximum_fusion.14, bf16[]{:T(256)} %bitcast.127, bf16[]{:T(256)} %bitcast.126, bf16[]{:T(256)} %bitcast.125, bf16[]{:T(256)} %bitcast.124, bf16[]{:T(256)} %bitcast.123, bf16[]{:T(256)} %bitcast.122, bf16[]{:T(256)} %bitcast.121, bf16[]{:T(256)} %bitcast.120, ...), kind=kOutput, calls=%fused_computation.61 | convolution fusion | flops 33508864 | bytes 565282 | tf_op jit(solution)/shard_map/abc,bw->awc/dot_general | solution.py:77
  643.7 10.8 %fusion.72 = f32[32,32,64]{2,0,1:T(8,128)S(1)} fusion(bf16[48,32,64]{2,1,0:T(8,128)(2,1)S(1)} %fusion.35, bf16[]{:T(256)} %bitcast.127, bf16[]{:T(256)} %bitcast.126, bf16[]{:T(256)} %bitcast.125, bf16[]{:T(256)} %bitcast.124, bf16[]{:T(256)} %bitcast.123, bf16[]{:T(256)} %bitcast.122, bf16[]{:T(256)} %bitcast.121, bf16[]{:T(256)} %bitcast.120, ...), kind=kOutput, calls=%fused_computation.145 | convolution fusion | flops 6345216 | bytes 458786 | tf_op jit(solution)/shard_map/abc,aw->wbc/dot_general | solution.py:77
  654.5 11.3 %fusion.34 = bf16[48,32,64]{2,1,0:T(8,128)(2,1)S(1)} fusion(bf16[48,48,80]{2,1,0:T(8,128)(2,1)S(1)} %pad_maximum_fusion.14, bf16[]{:T(256)} %bitcast.164, bf16[]{:T(256)} %bitcast.163, bf16[]{:T(256)} %bitcast.162, bf16[]{:T(256)} %bitcast.161, bf16[]{:T(256)} %bitcast.160, bf16[]{:T(256)} %bitcast.159, bf16[]{:T(256)} %bitcast.158, bf16[]{:T(256)} %bitcast.157, ...), kind=kOutput, calls=%fused_computation.60 | convolution fusion | flops 33508864 | bytes 565282 | tf_op jit(solution)/shard_map/abc,bw->awc/dot_general | solution.py:77
  665.8 11.0 %convolution_add_fusion.2 = f32[32,32,64]{2,0,1:T(8,128)S(1)} fusion(f32[32,32,64]{2,0,1:T(8,128)S(1)} %fusion.72, bf16[48,32,64]{2,1,0:T(8,128)(2,1)S(1)} %fusion.34, bf16[]{:T(256)} %bitcast.164, bf16[]{:T(256)} %bitcast.163, bf16[]{:T(256)} %bitcast.162, bf16[]{:T(256)} %bitcast.161, bf16[]{:T(256)} %bitcast.160, bf16[]{:T(256)} %bitcast.159, ...), kind=kOutput, calls=%fused_computation.57 | convolution fusion | flops 6410752 | bytes 720930 | tf_op jit(solution)/shard_map/abc,aw->wbc/dot_general | solution.py:77
  676.8 11.2 %fusion.33 = bf16[48,32,64]{2,1,0:T(8,128)(2,1)S(1)} fusion(bf16[48,48,80]{2,1,0:T(8,128)(2,1)S(1)} %pad_maximum_fusion.14, bf16[]{:T(256)} %bitcast.201, bf16[]{:T(256)} %bitcast.200, bf16[]{:T(256)} %bitcast.199, bf16[]{:T(256)} %bitcast.198, bf16[]{:T(256)} %bitcast.197, bf16[]{:T(256)} %bitcast.196, bf16[]{:T(256)} %bitcast.195, bf16[]{:T(256)} %bitcast.194, ...), kind=kOutput, calls=%fused_computation.59 | convolution fusion | flops 33508864 | bytes 565282 | tf_op jit(solution)/shard_map/abc,bw->awc/dot_general | solution.py:77
  688.1 11.7 %convolution_add_fusion.1 = f32[32,32,64]{2,0,1:T(8,128)} fusion(f32[32,32,64]{2,0,1:T(8,128)S(1)} %convolution_add_fusion.2, bf16[48,32,64]{2,1,0:T(8,128)(2,1)S(1)} %fusion.33, bf16[]{:T(256)} %bitcast.201, bf16[]{:T(256)} %bitcast.200, bf16[]{:T(256)} %bitcast.199, bf16[]{:T(256)} %bitcast.198, bf16[]{:T(256)} %bitcast.197, bf16[]{:T(256)} %bitcast.196, ...), kind=kOutput, calls=%fused_computation.56 | convolution fusion | flops 6410752 | bytes 720930 | tf_op jit(solution)/shard_map/abc,aw->wbc/dot_general | solution.py:77
  702.0 12.1 %fusion.32 = bf16[48,32,64]{2,1,0:T(8,128)(2,1)} fusion(bf16[48,48,80]{2,1,0:T(8,128)(2,1)S(1)} %pad_maximum_fusion.14, bf16[]{:T(256)} %bitcast.238, bf16[]{:T(256)} %bitcast.237, bf16[]{:T(256)} %bitcast.236, bf16[]{:T(256)} %bitcast.235, bf16[]{:T(256)} %bitcast.234, bf16[]{:T(256)} %bitcast.233, bf16[]{:T(256)} %bitcast.232, bf16[]{:T(256)} %bitcast.231, ...), kind=kOutput, calls=%fused_computation.58 | convolution fusion | flops 33508864 | bytes 565282 | tf_op jit(solution)/shard_map/abc,bw->awc/dot_general | solution.py:77
  717.5 12.2 %fusion.31 = f32[32,32,64]{2,0,1:T(8,128)S(1)} fusion(f32[32,32,64]{2,0,1:T(8,128)S(1)} %copy.206, f32[32,32,64]{2,0,1:T(8,128)} %convolution_add_fusion.1, bf16[48,32,64]{2,1,0:T(8,128)(2,1)} %fusion.32, bf16[]{:T(256)} %bitcast.238, bf16[]{:T(256)} %bitcast.237, bf16[]{:T(256)} %bitcast.236, bf16[]{:T(256)} %bitcast.235, bf16[]{:T(256)} %bitcast.234, ...), kind=kOutput, calls=%fused_computation.55 | convolution fusion | flops 6476288 | bytes 983074 | tf_op jit(solution)/shard_map/abc,aw->wbc/dot_general | solution.py:77
  733.6 13.0 %fusion.17 = f32[64,64,128]{2,0,1:T(8,128)} fusion(bf16[80,64,128]{2,1,0:T(8,128)(2,1)S(1)} %copy-done.6, bf16[]{:T(256)} %bitcast.617, bf16[]{:T(256)} %bitcast.616, bf16[]{:T(256)} %bitcast.615, bf16[]{:T(256)} %bitcast.614, bf16[]{:T(256)} %bitcast.613, bf16[]{:T(256)} %bitcast.612, bf16[]{:T(256)} %bitcast.611, bf16[]{:T(256)} %bitcast.610, ...), kind=kOutput, calls=%fused_computation.40 | convolution fusion | flops 84065280 | bytes 3407906 | tf_op jit(solution)/shard_map/abc,aw->wbc/dot_general | solution.py:77
  748.7 13.6 %fusion.19 = f32[64,64,128]{2,0,1:T(8,128)} fusion(bf16[80,64,128]{2,1,0:T(8,128)(2,1)S(1)} %copy-done.5, bf16[]{:T(256)} %bitcast.599, bf16[]{:T(256)} %bitcast.598, bf16[]{:T(256)} %bitcast.597, bf16[]{:T(256)} %bitcast.596, bf16[]{:T(256)} %bitcast.595, bf16[]{:T(256)} %bitcast.594, bf16[]{:T(256)} %bitcast.593, bf16[]{:T(256)} %bitcast.592, ...), kind=kOutput, calls=%fused_computation.42 | convolution fusion | flops 84065280 | bytes 3407906 | tf_op jit(solution)/shard_map/abc,aw->wbc/dot_general | solution.py:77
  765.4 13.0 %fusion.21 = f32[64,64,128]{2,0,1:T(8,128)} fusion(bf16[80,64,128]{2,1,0:T(8,128)(2,1)S(1)} %copy-done.4, bf16[]{:T(256)} %bitcast.581, bf16[]{:T(256)} %bitcast.580, bf16[]{:T(256)} %bitcast.579, bf16[]{:T(256)} %bitcast.578, bf16[]{:T(256)} %bitcast.577, bf16[]{:T(256)} %bitcast.576, bf16[]{:T(256)} %bitcast.575, bf16[]{:T(256)} %bitcast.574, ...), kind=kOutput, calls=%fused_computation.44 | convolution fusion | flops 84065280 | bytes 3407906 | tf_op jit(solution)/shard_map/abc,aw->wbc/dot_general | solution.py:77
  797.3 14.8 %add_convert_fusion.4 = bf16[64,64,128]{2,0,1:T(8,128)(2,1)S(1)} fusion(f32[64,64,128]{2,0,1:T(8,128)S(1)} %copy.216, f32[64,64,128]{2,0,1:T(8,128)} %fusion.17, f32[64,64,128]{2,0,1:T(8,128)} %fusion.21, f32[64,64,128]{2,0,1:T(8,128)} %fusion.19, bf16[80,64,128]{2,1,0:T(8,128)(2,1)S(1)} %copy-done.3, bf16[]{:T(256)} %bitcast.635, bf16[]{:T(256)} %bitcast.634, ...), kind=kOutput, calls=%fused_computation.16 | convolution fusion | flops 86686720 | bytes 10747938 | tf_op jit(solution)/shard_map/abc,aw->wbc/dot_general | solution.py:77
  (334 shorter events, 376.6 us)
Async XLA Ops:
  1.5 67.4 %collective-permute-start.6 = (f32[3,64,128]{2,1,0:T(8,128)}, f32[3,64,128]{2,1,0:T(8,128)S(1)}, u32[]{:S(2)}, u32[]{:S(2)}) collective-permute-start(f32[3,64,128]{2,1,0:T(8,128)} %get-tuple-element.25), channel_id=1, source_target_pairs={{0,8},{8,16},{16,24},{24,0},{1,9},{9,17},{17,25},{25,1},{2,10},{10... | collective-permute-start | bytes 294920 | tf_op jit(solution)/shard_map/ppermute | solution.py:14
  4.6 64.3 %collective-permute-start.7 = (f32[3,64,128]{2,1,0:T(8,128)}, f32[3,64,128]{2,1,0:T(8,128)}, u32[]{:S(2)}, u32[]{:S(2)}) collective-permute-start(f32[3,64,128]{2,1,0:T(8,128)} %get-tuple-element.26), channel_id=1, source_target_pairs={{8,0},{16,8},{24,16},{0,24},{9,1},{17,9},{25,17},{1,25},{10,2},{18... | collective-permute-start | bytes 294920 | tf_op jit(solution)/shard_map/ppermute | solution.py:15
  8.2 63.2 %collective-permute-start.1 = (bf16[8,64,128]{2,1,0:T(8,128)(2,1)}, bf16[8,64,128]{2,1,0:T(8,128)(2,1)}, u32[]{:S(2)}, u32[]{:S(2)}) collective-permute-start(bf16[8,64,128]{2,1,0:T(8,128)(2,1)} %get-tuple-element.21), channel_id=1, source_target_pairs={{8,0},{16,8},{24,16},{0,24},{9,1},{17,9},{25,17},{1,25},{10,2},{18... | collective-permute-start | bytes 393224 | tf_op jit(solution)/shard_map/ppermute | solution.py:15
  10.3 56.6 %collective-permute-start = (bf16[8,64,128]{2,1,0:T(8,128)(2,1)S(1)}, bf16[8,64,128]{2,1,0:T(8,128)(2,1)S(1)}, u32[]{:S(2)}, u32[]{:S(2)}) collective-permute-start(bf16[8,64,128]{2,1,0:T(8,128)(2,1)S(1)} %get-tuple-element.22), channel_id=1, source_target_pairs={{0,8},{8,16},{16,24},{24,0},{1,9},{9,17},{17,25},{25,1},{2,10},{10... | collective-permute-start | bytes 393224 | tf_op jit(solution)/shard_map/ppermute | solution.py:14
  73.3 16.0 %collective-permute-start.2 = (bf16[80,8,128]{2,1,0:T(8,128)(2,1)}, bf16[80,8,128]{2,1,0:T(8,128)(2,1)}, u32[]{:S(2)}, u32[]{:S(2)}) collective-permute-start(bf16[80,8,128]{2,1,0:T(8,128)(2,1)} %get-tuple-element.17), channel_id=1, source_target_pairs={{0,2},{2,4},{4,6},{6,0},{1,3},{3,5},{5,7},{7,1},{8,10},{10,12},{12... | collective-permute-start | bytes 491528 | tf_op jit(solution)/shard_map/ppermute | solution.py:14
  73.4 15.9 %collective-permute-start.3 = (bf16[80,8,128]{2,1,0:T(8,128)(2,1)}, bf16[80,8,128]{2,1,0:T(8,128)(2,1)}, u32[]{:S(2)}, u32[]{:S(2)}) collective-permute-start(bf16[80,8,128]{2,1,0:T(8,128)(2,1)} %get-tuple-element.18), channel_id=1, source_target_pairs={{2,0},{4,2},{6,4},{0,6},{3,1},{5,3},{7,5},{1,7},{10,8},{12,10},{14... | collective-permute-start | bytes 491528 | tf_op jit(solution)/shard_map/ppermute | solution.py:15
  87.3 11.3 %collective-permute-start.11 = (f32[70,70,3]{1,0,2:T(8,128)}, f32[70,70,3]{1,0,2:T(8,128)}, u32[]{:S(2)}, u32[]{:S(2)}) collective-permute-start(f32[70,70,3]{1,0,2:T(8,128)} %copy.167), channel_id=1, source_target_pairs={{1,0},{0,1},{3,2},{2,3},{5,4},{4,5},{7,6},{6,7},{9,8},{8,9},{11,10... | collective-permute-start | bytes 176408 | tf_op jit(solution)/shard_map/ppermute | solution.py:15
  182.4 11.9 %collective-permute-start.18 = (f32[3,32,64]{2,1,0:T(8,128)S(1)}, f32[3,32,64]{2,1,0:T(8,128)S(1)}, u32[]{:S(2)}, u32[]{:S(2)}) collective-permute-start(f32[3,32,64]{2,1,0:T(8,128)S(1)} %get-tuple-element.45), channel_id=1, source_target_pairs={{0,8},{8,16},{16,24},{24,0},{1,9},{9,17},{17,25},{25,1},{2,10},{10... | collective-permute-start | bytes 73736 | tf_op jit(solution)/shard_map/ppermute | solution.py:14
  182.5 11.8 %collective-permute-start.19 = (f32[3,32,64]{2,1,0:T(8,128)S(1)}, f32[3,32,64]{2,1,0:T(8,128)S(1)}, u32[]{:S(2)}, u32[]{:S(2)}) collective-permute-start(f32[3,32,64]{2,1,0:T(8,128)S(1)} %get-tuple-element.46), channel_id=1, source_target_pairs={{8,0},{16,8},{24,16},{0,24},{9,1},{17,9},{25,17},{1,25},{10,2},{18... | collective-permute-start | bytes 73736 | tf_op jit(solution)/shard_map/ppermute | solution.py:15
  192.3 267.4 %collective-permute-start.5 = (bf16[80,80,8]{1,2,0:T(8,128)(2,1)}, bf16[80,80,8]{1,2,0:T(8,128)(2,1)}, u32[]{:S(2)}, u32[]{:S(2)}) collective-permute-start(bf16[80,80,8]{1,2,0:T(8,128)(2,1)} %copy.150), channel_id=1, source_target_pairs={{1,0},{0,1},{3,2},{2,3},{5,4},{4,5},{7,6},{6,7},{9,8},{8,9},{11,10... | collective-permute-start | bytes 307208 | tf_op jit(solution)/shard_map/ppermute | solution.py:15
  193.8 263.5 %collective-permute-start.4 = (bf16[80,80,8]{1,2,0:T(8,128)(2,1)}, bf16[80,80,8]{1,2,0:T(8,128)(2,1)}, u32[]{:S(2)}, u32[]{:S(2)}) collective-permute-start(bf16[80,80,8]{1,2,0:T(8,128)(2,1)} %copy.149), channel_id=1, source_target_pairs={{0,1},{1,0},{2,3},{3,2},{4,5},{5,4},{6,7},{7,6},{8,9},{9,8},{10,11... | collective-permute-start | bytes 307208 | tf_op jit(solution)/shard_map/ppermute | solution.py:14
  204.0 24.3 %collective-permute-start.14 = (bf16[48,8,64]{2,1,0:T(8,128)(2,1)S(1)}, bf16[48,8,64]{2,1,0:T(8,128)(2,1)S(1)}, u32[]{:S(2)}, u32[]{:S(2)}) collective-permute-start(bf16[48,8,64]{2,1,0:T(8,128)(2,1)S(1)} %get-tuple-element.49), channel_id=1, source_target_pairs={{0,2},{2,4},{4,6},{6,0},{1,3},{3,5},{5,7},{7,1},{8,10},{10,12},{12... | collective-permute-start | bytes 147464 | tf_op jit(solution)/shard_map/ppermute | solution.py:14
  229.6 223.8 %collective-permute-start.26 = (bf16[32,8,32]{2,1,0:T(8,128)(2,1)}, bf16[32,8,32]{2,1,0:T(8,128)(2,1)}, u32[]{:S(2)}, u32[]{:S(2)}) collective-permute-start(bf16[32,8,32]{2,1,0:T(8,128)(2,1)} %get-tuple-element.71), channel_id=1, source_target_pairs={{0,2},{2,4},{4,6},{6,0},{1,3},{3,5},{5,7},{7,1},{8,10},{10,12},{12... | collective-permute-start | bytes 49160 | tf_op jit(solution)/shard_map/ppermute | solution.py:14
  231.5 9.2 %collective-permute-start.34 = (f32[22,22,3]{2,1,0:T(8,128)S(1)}, f32[22,22,3]{2,1,0:T(8,128)S(1)}, u32[]{:S(2)}, u32[]{:S(2)}) collective-permute-start(f32[22,22,3]{2,1,0:T(8,128)S(1)} %get-tuple-element.53), channel_id=1, source_target_pairs={{0,1},{1,0},{2,3},{3,2},{4,5},{5,4},{6,7},{7,6},{8,9},{9,8},{10,11... | collective-permute-start | bytes 17432 | tf_op jit(solution)/shard_map/ppermute | solution.py:14
  232.7 13.8 %collective-permute-start.35 = (f32[22,22,3]{2,1,0:T(8,128)S(1)}, f32[22,22,3]{2,1,0:T(8,128)S(1)}, u32[]{:S(2)}, u32[]{:S(2)}) collective-permute-start(f32[22,22,3]{2,1,0:T(8,128)S(1)} %get-tuple-element.54), channel_id=1, source_target_pairs={{1,0},{0,1},{3,2},{2,3},{5,4},{4,5},{7,6},{6,7},{9,8},{8,9},{11,10... | collective-permute-start | bytes 17432 | tf_op jit(solution)/shard_map/ppermute | solution.py:15
  240.7 212.7 %collective-permute-start.27 = (bf16[32,8,32]{2,1,0:T(8,128)(2,1)}, bf16[32,8,32]{2,1,0:T(8,128)(2,1)}, u32[]{:S(2)}, u32[]{:S(2)}) collective-permute-start(bf16[32,8,32]{2,1,0:T(8,128)(2,1)} %get-tuple-element.72), channel_id=1, source_target_pairs={{2,0},{4,2},{6,4},{0,6},{3,1},{5,3},{7,5},{1,7},{10,8},{12,10},{14... | collective-permute-start | bytes 49160 | tf_op jit(solution)/shard_map/ppermute | solution.py:15
  246.5 384.2 %collective-permute-start.17 = (bf16[48,48,8]{1,2,0:T(8,128)(2,1)}, bf16[48,48,8]{1,2,0:T(8,128)(2,1)}, u32[]{:S(2)}, u32[]{:S(2)}) collective-permute-start(bf16[48,48,8]{1,2,0:T(8,128)(2,1)} %copy.171), channel_id=1, source_target_pairs={{1,0},{0,1},{3,2},{2,3},{5,4},{4,5},{7,6},{6,7},{9,8},{8,9},{11,10... | collective-permute-start | bytes 110600 | tf_op jit(solution)/shard_map/ppermute | solution.py:15
  453.4 176.0 %collective-permute-start.16 = (bf16[48,48,8]{1,2,0:T(8,128)(2,1)}, bf16[48,48,8]{1,2,0:T(8,128)(2,1)}, u32[]{:S(2)}, u32[]{:S(2)}) collective-permute-start(bf16[48,48,8]{1,2,0:T(8,128)(2,1)} %copy.170), channel_id=1, source_target_pairs={{0,1},{1,0},{2,3},{3,2},{4,5},{5,4},{6,7},{7,6},{8,9},{9,8},{10,11... | collective-permute-start | bytes 110600 | tf_op jit(solution)/shard_map/ppermute | solution.py:14
  455.3 63.3 %collective-permute-start.28 = (bf16[32,32,8]{2,1,0:T(8,128)(2,1)}, bf16[32,32,8]{2,1,0:T(8,128)(2,1)}, u32[]{:S(2)}, u32[]{:S(2)}) collective-permute-start(bf16[32,32,8]{2,1,0:T(8,128)(2,1)} %get-tuple-element.57), channel_id=1, source_target_pairs={{0,1},{1,0},{2,3},{3,2},{4,5},{5,4},{6,7},{7,6},{8,9},{9,8},{10,11... | collective-permute-start | bytes 49160 | tf_op jit(solution)/shard_map/ppermute | solution.py:14
  457.3 61.3 %collective-permute-start.29 = (bf16[32,32,8]{2,1,0:T(8,128)(2,1)}, bf16[32,32,8]{2,1,0:T(8,128)(2,1)}, u32[]{:S(2)}, u32[]{:S(2)}) collective-permute-start(bf16[32,32,8]{2,1,0:T(8,128)(2,1)} %get-tuple-element.58), channel_id=1, source_target_pairs={{1,0},{0,1},{3,2},{2,3},{5,4},{4,5},{7,6},{6,7},{9,8},{8,9},{11,10... | collective-permute-start | bytes 49160 | tf_op jit(solution)/shard_map/ppermute | solution.py:15
  611.0 16.7 %collective-permute-start.36 = (f32[2,16,32]{2,0,1:T(2,128)S(1)}, f32[2,16,32]{2,0,1:T(2,128)S(1)}, u32[]{:S(2)}, u32[]{:S(2)}) collective-permute-start(f32[2,16,32]{2,0,1:T(2,128)S(1)} %get-tuple-element.69), channel_id=1, source_target_pairs={{0,8},{8,16},{16,24},{24,0},{1,9},{9,17},{17,25},{25,1},{2,10},{10... | collective-permute-start | bytes 12296 | tf_op jit(solution)/shard_map/ppermute | solution.py:14
  611.1 16.6 %collective-permute-start.37 = (f32[2,16,32]{2,0,1:T(2,128)S(1)}, f32[2,16,32]{2,0,1:T(2,128)S(1)}, u32[]{:S(2)}, u32[]{:S(2)}) collective-permute-start(f32[2,16,32]{2,0,1:T(2,128)S(1)} %get-tuple-element.70), channel_id=1, source_target_pairs={{8,0},{16,8},{24,16},{0,24},{9,1},{17,9},{25,17},{1,25},{10,2},{18... | collective-permute-start | bytes 12296 | tf_op jit(solution)/shard_map/ppermute | solution.py:15
  627.7 72.0 %collective-permute-start.38 = (f32[20,2,32]{2,0,1:T(8,128)S(1)}, f32[20,2,32]{2,0,1:T(8,128)S(1)}, u32[]{:S(2)}, u32[]{:S(2)}) collective-permute-start(f32[20,2,32]{2,0,1:T(8,128)S(1)} %get-tuple-element.67), channel_id=1, source_target_pairs={{0,2},{2,4},{4,6},{6,0},{1,3},{3,5},{5,7},{7,1},{8,10},{10,12},{12... | collective-permute-start | bytes 15368 | tf_op jit(solution)/shard_map/ppermute | solution.py:14
  627.8 72.0 %collective-permute-start.39 = (f32[20,2,32]{2,0,1:T(8,128)S(1)}, f32[20,2,32]{2,0,1:T(8,128)S(1)}, u32[]{:S(2)}, u32[]{:S(2)}) collective-permute-start(f32[20,2,32]{2,0,1:T(8,128)S(1)} %get-tuple-element.68), channel_id=1, source_target_pairs={{2,0},{4,2},{6,4},{0,6},{3,1},{5,3},{7,5},{1,7},{10,8},{12,10},{14... | collective-permute-start | bytes 15368 | tf_op jit(solution)/shard_map/ppermute | solution.py:15
  699.9 14.2 %collective-permute-start.40 = (f32[20,20,2]{2,0,1:T(8,128)S(1)}, f32[20,20,2]{2,0,1:T(8,128)S(1)}, u32[]{:S(2)}, u32[]{:S(2)}) collective-permute-start(f32[20,20,2]{2,0,1:T(8,128)S(1)} %get-tuple-element.63), channel_id=1, source_target_pairs={{0,1},{1,0},{2,3},{3,2},{4,5},{5,4},{6,7},{7,6},{8,9},{9,8},{10,11... | collective-permute-start | bytes 9608 | tf_op jit(solution)/shard_map/ppermute | solution.py:14
  702.0 12.2 %collective-permute-start.41 = (f32[20,20,2]{2,0,1:T(8,128)S(1)}, f32[20,20,2]{2,0,1:T(8,128)S(1)}, u32[]{:S(2)}, u32[]{:S(2)}) collective-permute-start(f32[20,20,2]{2,0,1:T(8,128)S(1)} %get-tuple-element.64), channel_id=1, source_target_pairs={{1,0},{0,1},{3,2},{2,3},{5,4},{4,5},{7,6},{6,7},{9,8},{8,9},{11,10... | collective-permute-start | bytes 9608 | tf_op jit(solution)/shard_map/ppermute | solution.py:15
  729.7 16.9 %collective-permute-start.42 = (f32[2,32,64]{2,0,1:T(2,128)S(1)}, f32[2,32,64]{2,0,1:T(2,128)S(1)}, u32[]{:S(2)}, u32[]{:S(2)}) collective-permute-start(f32[2,32,64]{2,0,1:T(2,128)S(1)} %get-tuple-element.41), channel_id=1, source_target_pairs={{0,8},{8,16},{16,24},{24,0},{1,9},{9,17},{17,25},{25,1},{2,10},{10... | collective-permute-start | bytes 49160 | tf_op jit(solution)/shard_map/ppermute | solution.py:14
  729.8 16.9 %collective-permute-start.43 = (f32[2,32,64]{2,0,1:T(2,128)S(1)}, f32[2,32,64]{2,0,1:T(2,128)S(1)}, u32[]{:S(2)}, u32[]{:S(2)}) collective-permute-start(f32[2,32,64]{2,0,1:T(2,128)S(1)} %get-tuple-element.42), channel_id=1, source_target_pairs={{8,0},{16,8},{24,16},{0,24},{9,1},{17,9},{25,17},{1,25},{10,2},{18... | collective-permute-start | bytes 49160 | tf_op jit(solution)/shard_map/ppermute | solution.py:15
  746.7 15.6 %collective-permute-start.44 = (f32[36,2,64]{2,0,1:T(8,128)S(1)}, f32[36,2,64]{2,0,1:T(8,128)S(1)}, u32[]{:S(2)}, u32[]{:S(2)}) collective-permute-start(f32[36,2,64]{2,0,1:T(8,128)S(1)} %get-tuple-element.37), channel_id=1, source_target_pairs={{0,2},{2,4},{4,6},{6,0},{1,3},{3,5},{5,7},{7,1},{8,10},{10,12},{12... | collective-permute-start | bytes 55304 | tf_op jit(solution)/shard_map/ppermute | solution.py:14
  746.7 15.5 %collective-permute-start.45 = (f32[36,2,64]{2,0,1:T(8,128)S(1)}, f32[36,2,64]{2,0,1:T(8,128)S(1)}, u32[]{:S(2)}, u32[]{:S(2)}) collective-permute-start(f32[36,2,64]{2,0,1:T(8,128)S(1)} %get-tuple-element.38), channel_id=1, source_target_pairs={{2,0},{4,2},{6,4},{0,6},{3,1},{5,3},{7,5},{1,7},{10,8},{12,10},{14... | collective-permute-start | bytes 55304 | tf_op jit(solution)/shard_map/ppermute | solution.py:15
  763.3 15.5 %collective-permute-start.47 = (f32[36,36,2]{1,2,0:T(2,128)S(1)}, f32[36,36,2]{1,2,0:T(2,128)S(1)}, u32[]{:S(2)}, u32[]{:S(2)}) collective-permute-start(f32[36,36,2]{1,2,0:T(2,128)S(1)} %copy.208), channel_id=1, source_target_pairs={{1,0},{0,1},{3,2},{2,3},{5,4},{4,5},{7,6},{6,7},{9,8},{8,9},{11,10... | collective-permute-start | bytes 31112 | tf_op jit(solution)/shard_map/ppermute | solution.py:15
  765.3 13.1 %collective-permute-start.46 = (f32[36,36,2]{1,2,0:T(2,128)S(1)}, f32[36,36,2]{1,2,0:T(2,128)S(1)}, u32[]{:S(2)}, u32[]{:S(2)}) collective-permute-start(f32[36,36,2]{1,2,0:T(2,128)S(1)} %copy.207), channel_id=1, source_target_pairs={{0,1},{1,0},{2,3},{3,2},{4,5},{5,4},{6,7},{7,6},{8,9},{9,8},{10,11... | collective-permute-start | bytes 31112 | tf_op jit(solution)/shard_map/ppermute | solution.py:14
  (45 other events, 1153.5 us)
where the time goes:
time: 826 us; the launch traced here: 814 us
  matrix products  425 us (51%)
  local copies, waits for them, and re-layouts  155 us (19%)
  other arithmetic  84 us (10%)
  blocking collectives  68.6 us (8%)
  starting transfers between devices  58.2 us (7%)
  waiting for transfers between devices  22.3 us (3%)
    dot_general x36, matrix products, pass_along(): jnp.einsum(letters + ',' + letters[along] + 'w->' + target, padded, matri...  418 us
    slice x30, local copies, waits for them, and re-layouts, strided(): lax.slice_in_dim(padded, 3 + offset, 3 + offset + fine_count, 2, along)  75.9 us
    all_gather x1, blocking collectives, per_device(): lax.all_gather(level_three.astype(jnp.bfloat16).reshape(1, block_x * bloc...  68.6 us
    ppermute x24, starting transfers between devices, padded_2(): after = lax.ppermute(first, axis, down)  45 us
    convert_element_type x4, other arithmetic, band(): return matrix.astype(jnp.bfloat16)  44.9 us
    concatenate x17, other arithmetic, padded_2(): value = jnp.concatenate([before, value, after], axis=dim)  20.3 us
    slice x22, local copies, waits for them, and re-layouts, padded_2(): last = lax.slice_in_dim(value, length - width, length, axis=dim)  17.6 us
    ppermute x24, waiting for transfers between devices, padded_2(): before = lax.ppermute(last, axis, up)  17.5 us
  transfers between devices with their start and end apart: 48, of which 7 were waited for; matrix products, arithmetic and copies ran while one was open for 65% of the time, Pallas kernels for 0%

commit v1 on v0

--- a/solution.py
+++ b/solution.py
@@ -134,12 +134,9 @@
     count_x = lax.axis_size("gx")
     count_y = lax.axis_size("gy")
     count_z = lax.axis_size("gz")
-    pieces = lax.all_gather(
-        level_three.astype(jnp.bfloat16).reshape(1, block_x * block_y * block_z),
-        ("gx", "gy", "gz"),
-        axis=0,
-        tiled=True,
-    )
+    own = level_three.astype(jnp.bfloat16).reshape(1, block_x * block_y * block_z)
+    outgoing = jnp.stack([own] * lax.axis_size(("gx", "gy", "gz")))
+    pieces = jnp.concatenate(lax.all_to_all(outgoing, ("gx", "gy", "gz"), 0, 0), axis=0)
     top_grid = pieces.reshape(count_x, count_y, count_z, block_x, block_y, block_z).transpose(
         0, 3, 1, 4, 2, 5
     )

time: 826 us -> 773 us (0.936)
  blocking collectives: 68.6 us -> 0 us
    all_gather x1 -> x0, blocking collectives: 68.6 us -> none  [per_device(): lax.all_gather(level_three.astype(jnp.bfloat16).reshape(1, block_x * bloc...]
  transfers between devices with their start and end apart: 48 -> 49, of which waited for: 7 -> 8; matrix products, arithmetic and copies ran while one was open for 65% -> 50% of each run, Pallas kernels for 0% -> 0%
where the time goes in v1:
time: 773 us; the launch traced here: 761 us
  matrix products  423 us (55%)
  local copies, waits for them, and re-layouts  163 us (21%)
  other arithmetic  84.7 us (11%)
  starting transfers between devices  64 us (8%)
  waiting for transfers between devices  24 us (3%)
    dot_general x36, matrix products, pass_along(): jnp.einsum(letters + ',' + letters[along] + 'w->' + target, padded, matri...  416 us
    slice x30, local copies, waits for them, and re-layouts, strided(): lax.slice_in_dim(padded, 3 + offset, 3 + offset + fine_count, 2, along)  75.8 us
    convert_element_type x4, other arithmetic, band(): return matrix.astype(jnp.bfloat16)  44.6 us
    ppermute x24, starting transfers between devices, padded_2(): after = lax.ppermute(first, axis, down)  44.1 us
    concatenate x17, other arithmetic, padded_2(): value = jnp.concatenate([before, value, after], axis=dim)  20.3 us
    slice x22, local copies, waits for them, and re-layouts, padded_2(): last = lax.slice_in_dim(value, length - width, length, axis=dim)  19 us
    ppermute x24, waiting for transfers between devices, padded_2(): before = lax.ppermute(last, axis, up)  17.9 us
  transfers between devices with their start and end apart: 49, of which 8 were waited for; matrix products, arithmetic and copies ran while one was open for 50% of the time, Pallas kernels for 0%

profile of v1, /device:TPU:0, one launch (start us, length us, event | category | flops | bytes accessed | tf_op | source)
XLA Modules:
  0.0 760.6 jit_solution(2187248637277075908)
XLA Ops:
  31.2 11.4 %select_convert_fusion.5 = bf16[80,64]{0,1:T(8,128)(2,1)} fusion(bf16[]{:T(256)} %bitcast.617, bf16[]{:T(256)} %bitcast.616, bf16[]{:T(256)} %bitcast.615, bf16[]{:T(256)} %bitcast.614, bf16[]{:T(256)} %bitcast.613, bf16[]{:T(256)} %bitcast.612, bf16[]{:T(256)} %bitcast.611, bf16[]{:T(256)} %bitcast.610, bf16[]{:T(256)} %bitcast.609, bf16[]{:T(256)} %bitcast.608, ...), kind=kLoop, calls=%fused_computation.239 | loop fusion | flops 179200 | bytes 10274 | tf_op jit(solution)/shard_map/convert_element_type | solution.py:59
  42.5 11.2 %select_convert_fusion.6 = bf16[80,64]{0,1:T(8,128)(2,1)} fusion(bf16[]{:T(256)} %bitcast.599, bf16[]{:T(256)} %bitcast.598, bf16[]{:T(256)} %bitcast.597, bf16[]{:T(256)} %bitcast.596, bf16[]{:T(256)} %bitcast.595, bf16[]{:T(256)} %bitcast.594, bf16[]{:T(256)} %bitcast.593, bf16[]{:T(256)} %bitcast.592, bf16[]{:T(256)} %bitcast.591, bf16[]{:T(256)} %bitcast.590, ...), kind=kLoop, calls=%fused_computation.240 | loop fusion | flops 179200 | bytes 10274 | tf_op jit(solution)/shard_map/convert_element_type | solution.py:59
  53.7 11.2 %select_convert_fusion.7 = bf16[80,64]{0,1:T(8,128)(2,1)} fusion(bf16[]{:T(256)} %bitcast.581, bf16[]{:T(256)} %bitcast.580, bf16[]{:T(256)} %bitcast.579, bf16[]{:T(256)} %bitcast.578, bf16[]{:T(256)} %bitcast.577, bf16[]{:T(256)} %bitcast.576, bf16[]{:T(256)} %bitcast.575, bf16[]{:T(256)} %bitcast.574, bf16[]{:T(256)} %bitcast.573, bf16[]{:T(256)} %bitcast.572, ...), kind=kLoop, calls=%fused_computation.241 | loop fusion | flops 179200 | bytes 10274 | tf_op jit(solution)/shard_map/convert_element_type | solution.py:59
  278.1 12.8 %fusion.14 = bf16[80,64,128]{2,1,0:T(8,128)(2,1)} fusion(bf16[80,80,128]{1,2,0:T(8,128)(2,1)S(1)} %bitcast.800, bf16[]{:T(256)} %bitcast.617, bf16[]{:T(256)} %bitcast.616, bf16[]{:T(256)} %bitcast.615, bf16[]{:T(256)} %bitcast.614, bf16[]{:T(256)} %bitcast.613, bf16[]{:T(256)} %bitcast.612, bf16[]{:T(256)} %bitcast.611, bf16[]{:T(256)} %bitcast.610, ...), kind=kOutput, calls=%fused_computation.33 | convolution fusion | flops 105692160 | bytes 2949154 | tf_op jit(solution)/shard_map/abc,bw->awc/dot_general | solution.py:77
  292.6 12.8 %fusion.13 = bf16[80,64,128]{2,1,0:T(8,128)(2,1)} fusion(bf16[80,80,128]{1,2,0:T(8,128)(2,1)S(1)} %bitcast.801, bf16[]{:T(256)} %bitcast.599, bf16[]{:T(256)} %bitcast.598, bf16[]{:T(256)} %bitcast.597, bf16[]{:T(256)} %bitcast.596, bf16[]{:T(256)} %bitcast.595, bf16[]{:T(256)} %bitcast.594, bf16[]{:T(256)} %bitcast.593, bf16[]{:T(256)} %bitcast.592, ...), kind=kOutput, calls=%fused_computation.32 | convolution fusion | flops 105692160 | bytes 2949154 | tf_op jit(solution)/shard_map/abc,bw->awc/dot_general | solution.py:77
  307.1 11.6 %fusion.12 = bf16[80,64,128]{2,1,0:T(8,128)(2,1)S(1)} fusion(bf16[80,80,128]{1,2,0:T(8,128)(2,1)S(1)} %bitcast.802, bf16[]{:T(256)} %bitcast.581, bf16[]{:T(256)} %bitcast.580, bf16[]{:T(256)} %bitcast.579, bf16[]{:T(256)} %bitcast.578, bf16[]{:T(256)} %bitcast.577, bf16[]{:T(256)} %bitcast.576, bf16[]{:T(256)} %bitcast.575, bf16[]{:T(256)} %bitcast.574, ...), kind=kOutput, calls=%fused_computation.31 | convolution fusion | flops 105692160 | bytes 2949154 | tf_op jit(solution)/shard_map/abc,bw->awc/dot_general | solution.py:77
  320.4 12.9 %fusion.15 = bf16[80,64,128]{2,1,0:T(8,128)(2,1)} fusion(bf16[80,80,128]{1,2,0:T(8,128)(2,1)S(1)} %bitcast.799, bf16[]{:T(256)} %bitcast.635, bf16[]{:T(256)} %bitcast.634, bf16[]{:T(256)} %bitcast.633, bf16[]{:T(256)} %bitcast.632, bf16[]{:T(256)} %bitcast.631, bf16[]{:T(256)} %bitcast.630, bf16[]{:T(256)} %bitcast.629, bf16[]{:T(256)} %bitcast.628, ...), kind=kOutput, calls=%fused_computation.34 | convolution fusion | flops 105692160 | bytes 2949154 | tf_op jit(solution)/shard_map/abc,bw->awc/dot_general | solution.py:77
  334.7 11.1 %fusion.44 = bf16[32,16,32]{2,1,0:T(8,128)(2,1)S(1)} fusion(bf16[32,32,48]{2,1,0:T(8,128)(2,1)S(1)} %pad_maximum_fusion.21, bf16[]{:T(256)} %bitcast.275, bf16[]{:T(256)} %bitcast.274, bf16[]{:T(256)} %bitcast.273, bf16[]{:T(256)} %bitcast.272, bf16[]{:T(256)} %bitcast.271, bf16[]{:T(256)} %bitcast.270, bf16[]{:T(256)} %bitcast.269, bf16[]{:T(256)} %bitcast.268, ...), kind=kOutput, calls=%fused_computation.79 | convolution fusion | flops 4315136 | bytes 131106 | tf_op jit(solution)/shard_map/abc,bw->awc/dot_general | solution.py:77
  356.6 11.0 %fusion.45 = bf16[32,16,32]{2,1,0:T(8,128)(2,1)S(1)} fusion(bf16[32,32,48]{2,1,0:T(8,128)(2,1)S(1)} %pad_maximum_fusion.21, bf16[]{:T(256)} %bitcast.312, bf16[]{:T(256)} %bitcast.311, bf16[]{:T(256)} %bitcast.310, bf16[]{:T(256)} %bitcast.309, bf16[]{:T(256)} %bitcast.308, bf16[]{:T(256)} %bitcast.307, bf16[]{:T(256)} %bitcast.306, bf16[]{:T(256)} %bitcast.305, ...), kind=kOutput, calls=%fused_computation.80 | convolution fusion | flops 4315136 | bytes 131106 | tf_op jit(solution)/shard_map/abc,bw->awc/dot_general | solution.py:77
  378.4 10.9 %fusion.46 = bf16[32,16,32]{2,1,0:T(8,128)(2,1)S(1)} fusion(bf16[32,32,48]{2,1,0:T(8,128)(2,1)S(1)} %pad_maximum_fusion.21, bf16[]{:T(256)} %bitcast.349, bf16[]{:T(256)} %bitcast.348, bf16[]{:T(256)} %bitcast.347, bf16[]{:T(256)} %bitcast.346, bf16[]{:T(256)} %bitcast.345, bf16[]{:T(256)} %bitcast.344, bf16[]{:T(256)} %bitcast.343, bf16[]{:T(256)} %bitcast.342, ...), kind=kOutput, calls=%fused_computation.81 | convolution fusion | flops 4315136 | bytes 131106 | tf_op jit(solution)/shard_map/abc,bw->awc/dot_general | solution.py:77
  389.3 11.3 %convolution_add_fusion.4 = f32[16,16,32]{2,0,1:T(8,128)} fusion(f32[16,16,32]{2,0,1:T(8,128)S(1)} %convolution_add_fusion.5, bf16[32,16,32]{2,1,0:T(8,128)(2,1)S(1)} %fusion.46, bf16[]{:T(256)} %bitcast.349, bf16[]{:T(256)} %bitcast.348, bf16[]{:T(256)} %bitcast.347, bf16[]{:T(256)} %bitcast.346, bf16[]{:T(256)} %bitcast.345, bf16[]{:T(256)} %bitcast.344, ...), kind=kOutput, calls=%fused_computation.84 | convolution fusion | flops 550400 | bytes 98338 | tf_op jit(solution)/shard_map/abc,aw->wbc/dot_general | solution.py:77
  400.6 11.9 %fusion.47 = bf16[32,16,32]{2,1,0:T(8,128)(2,1)} fusion(bf16[32,32,48]{2,1,0:T(8,128)(2,1)S(1)} %pad_maximum_fusion.21, bf16[]{:T(256)} %bitcast.386, bf16[]{:T(256)} %bitcast.385, bf16[]{:T(256)} %bitcast.384, bf16[]{:T(256)} %bitcast.383, bf16[]{:T(256)} %bitcast.382, bf16[]{:T(256)} %bitcast.381, bf16[]{:T(256)} %bitcast.380, bf16[]{:T(256)} %bitcast.379, ...), kind=kOutput, calls=%fused_computation.82 | convolution fusion | flops 4315136 | bytes 131106 | tf_op jit(solution)/shard_map/abc,bw->awc/dot_general | solution.py:77
  417.3 11.1 %fusion.35 = bf16[48,32,64]{2,1,0:T(8,128)(2,1)S(1)} fusion(bf16[48,48,80]{2,1,0:T(8,128)(2,1)S(1)} %pad_maximum_fusion.14, bf16[]{:T(256)} %bitcast.127, bf16[]{:T(256)} %bitcast.126, bf16[]{:T(256)} %bitcast.125, bf16[]{:T(256)} %bitcast.124, bf16[]{:T(256)} %bitcast.123, bf16[]{:T(256)} %bitcast.122, bf16[]{:T(256)} %bitcast.121, bf16[]{:T(256)} %bitcast.120, ...), kind=kOutput, calls=%fused_computation.61 | convolution fusion | flops 33508864 | bytes 565282 | tf_op jit(solution)/shard_map/abc,bw->awc/dot_general | solution.py:77
  439.1 11.8 %fusion.34 = bf16[48,32,64]{2,1,0:T(8,128)(2,1)} fusion(bf16[48,48,80]{2,1,0:T(8,128)(2,1)S(1)} %pad_maximum_fusion.14, bf16[]{:T(256)} %bitcast.164, bf16[]{:T(256)} %bitcast.163, bf16[]{:T(256)} %bitcast.162, bf16[]{:T(256)} %bitcast.161, bf16[]{:T(256)} %bitcast.160, bf16[]{:T(256)} %bitcast.159, bf16[]{:T(256)} %bitcast.158, bf16[]{:T(256)} %bitcast.157, ...), kind=kOutput, calls=%fused_computation.60 | convolution fusion | flops 33508864 | bytes 565282 | tf_op jit(solution)/shard_map/abc,bw->awc/dot_general | solution.py:77
  450.9 11.7 %convolution_add_fusion.2 = f32[32,32,64]{2,0,1:T(8,128)S(1)} fusion(f32[32,32,64]{2,0,1:T(8,128)S(1)} %fusion.72, bf16[48,32,64]{2,1,0:T(8,128)(2,1)} %fusion.34, bf16[]{:T(256)} %bitcast.164, bf16[]{:T(256)} %bitcast.163, bf16[]{:T(256)} %bitcast.162, bf16[]{:T(256)} %bitcast.161, bf16[]{:T(256)} %bitcast.160, bf16[]{:T(256)} %bitcast.159, ...), kind=kOutput, calls=%fused_computation.57 | convolution fusion | flops 6410752 | bytes 720930 | tf_op jit(solution)/shard_map/abc,aw->wbc/dot_general | solution.py:77
  470.0 11.1 %convolution_convert_fusion.13 = bf16[28,28,20]{1,2,0:T(8,128)(2,1)S(1)} fusion(bf16[28,28,36]{2,1,0:T(8,128)(2,1)S(1)} %fusion.79, bf16[]{:T(256)} %bitcast.498, bf16[]{:T(256)} %bitcast.497, bf16[]{:T(256)} %bitcast.496, bf16[]{:T(256)} %bitcast.495, bf16[]{:T(256)} %bitcast.494, bf16[]{:T(256)} %bitcast.493, bf16[]{:T(256)} %bitcast.492, bf16[]{:T(256)} %bitcast.491, ...), kind=kOutput, calls=%fused_computation.72 | convolution fusion | flops 1169840 | bytes 87842 | tf_op jit(solution)/shard_map/abc,cw->abw/dot_general | solution.py:77
  481.1 11.0 %fusion.51 = bf16[28,12,20]{0,1,2:T(8,128)(2,1)S(1)} fusion(bf16[28,28,20]{1,2,0:T(8,128)(2,1)S(1)} %convolution_convert_fusion.13, bf16[]{:T(256)} %bitcast.498, bf16[]{:T(256)} %bitcast.497, bf16[]{:T(256)} %bitcast.496, bf16[]{:T(256)} %bitcast.495, bf16[]{:T(256)} %bitcast.494, bf16[]{:T(256)} %bitcast.493, bf16[]{:T(256)} %bitcast.492, bf16[]{:T(256)} %bitcast.491, ...), kind=kOutput, calls=%fused_computation.96 | convolution fusion | flops 394800 | bytes 44834 | tf_op jit(solution)/shard_map/abc,bw->awc/dot_general | solution.py:77
  492.1 11.0 %convolution_convert_fusion.14 = bf16[28,28,20]{1,2,0:T(8,128)(2,1)S(1)} fusion(bf16[28,28,36]{2,1,0:T(8,128)(2,1)S(1)} %fusion.79, bf16[]{:T(256)} %bitcast.461, bf16[]{:T(256)} %bitcast.460, bf16[]{:T(256)} %bitcast.459, bf16[]{:T(256)} %bitcast.458, bf16[]{:T(256)} %bitcast.457, bf16[]{:T(256)} %bitcast.456, bf16[]{:T(256)} %bitcast.455, bf16[]{:T(256)} %bitcast.454, ...), kind=kOutput, calls=%fused_computation.73 | convolution fusion | flops 1169840 | bytes 87842 | tf_op jit(solution)/shard_map/abc,cw->abw/dot_general | solution.py:77
  503.2 10.9 %fusion.50 = bf16[28,12,20]{0,1,2:T(8,128)(2,1)S(1)} fusion(bf16[28,28,20]{1,2,0:T(8,128)(2,1)S(1)} %convolution_convert_fusion.14, bf16[]{:T(256)} %bitcast.461, bf16[]{:T(256)} %bitcast.460, bf16[]{:T(256)} %bitcast.459, bf16[]{:T(256)} %bitcast.458, bf16[]{:T(256)} %bitcast.457, bf16[]{:T(256)} %bitcast.456, bf16[]{:T(256)} %bitcast.455, bf16[]{:T(256)} %bitcast.454, ...), kind=kOutput, calls=%fused_computation.95 | convolution fusion | flops 394800 | bytes 44834 | tf_op jit(solution)/shard_map/abc,bw->awc/dot_general | solution.py:77
  514.1 11.0 %convolution_convert_fusion.15 = bf16[28,28,20]{1,2,0:T(8,128)(2,1)S(1)} fusion(bf16[28,28,36]{2,1,0:T(8,128)(2,1)S(1)} %fusion.79, bf16[]{:T(256)} %bitcast.424, bf16[]{:T(256)} %bitcast.423, bf16[]{:T(256)} %bitcast.422, bf16[]{:T(256)} %bitcast.421, bf16[]{:T(256)} %bitcast.420, bf16[]{:T(256)} %bitcast.419, bf16[]{:T(256)} %bitcast.418, bf16[]{:T(256)} %bitcast.417, ...), kind=kOutput, calls=%fused_computation.74 | convolution fusion | flops 1169840 | bytes 87842 | tf_op jit(solution)/shard_map/abc,cw->abw/dot_general | solution.py:77
  535.9 11.1 %convolution_convert_fusion.12 = bf16[28,28,20]{1,2,0:T(8,128)(2,1)S(1)} fusion(bf16[28,28,36]{2,1,0:T(8,128)(2,1)S(1)} %fusion.79, bf16[]{:T(256)} %bitcast.535, bf16[]{:T(256)} %bitcast.534, bf16[]{:T(256)} %bitcast.533, bf16[]{:T(256)} %bitcast.532, bf16[]{:T(256)} %bitcast.531, bf16[]{:T(256)} %bitcast.530, bf16[]{:T(256)} %bitcast.529, bf16[]{:T(256)} %bitcast.528, ...), kind=kOutput, calls=%fused_computation.71 | convolution fusion | flops 1169840 | bytes 87842 | tf_op jit(solution)/shard_map/abc,cw->abw/dot_general | solution.py:77
  547.0 11.0 %fusion.52 = bf16[28,12,20]{0,1,2:T(8,128)(2,1)S(1)} fusion(bf16[28,28,20]{1,2,0:T(8,128)(2,1)S(1)} %convolution_convert_fusion.12, bf16[]{:T(256)} %bitcast.535, bf16[]{:T(256)} %bitcast.534, bf16[]{:T(256)} %bitcast.533, bf16[]{:T(256)} %bitcast.532, bf16[]{:T(256)} %bitcast.531, bf16[]{:T(256)} %bitcast.530, bf16[]{:T(256)} %bitcast.529, bf16[]{:T(256)} %bitcast.528, ...), kind=kOutput, calls=%fused_computation.97 | convolution fusion | flops 394800 | bytes 44834 | tf_op jit(solution)/shard_map/abc,bw->awc/dot_general | solution.py:77
  568.8 10.9 %convolution_add_fusion.8 = f32[12,12,20]{2,0,1:T(8,128)S(1)} fusion(f32[12,12,20]{2,0,1:T(8,128)S(1)} %fusion.104, bf16[28,12,20]{0,1,2:T(8,128)(2,1)S(1)} %fusion.50, bf16[]{:T(256)} %bitcast.461, bf16[]{:T(256)} %bitcast.460, bf16[]{:T(256)} %bitcast.459, bf16[]{:T(256)} %bitcast.458, bf16[]{:T(256)} %bitcast.457, bf16[]{:T(256)} %bitcast.456, ...), kind=kOutput, calls=%fused_computation.93 | convolution fusion | flops 175920 | bytes 36514 | tf_op jit(solution)/shard_map/abc,aw->wbc/dot_general | solution.py:77
  579.7 10.9 %convolution_add_fusion.7 = f32[12,12,20]{2,0,1:T(8,128)S(1)} fusion(f32[12,12,20]{2,0,1:T(8,128)S(1)} %convolution_add_fusion.8, bf16[28,12,20]{0,1,2:T(8,128)(2,1)S(1)} %fusion.51, bf16[]{:T(256)} %bitcast.498, bf16[]{:T(256)} %bitcast.497, bf16[]{:T(256)} %bitcast.496, bf16[]{:T(256)} %bitcast.495, bf16[]{:T(256)} %bitcast.494, bf16[]{:T(256)} %bitcast.493, ...), kind=kOutput, calls=%fused_computation.92 | convolution fusion | flops 175920 | bytes 36514 | tf_op jit(solution)/shard_map/abc,aw->wbc/dot_general | solution.py:77
  617.1 11.1 %fusion.33 = bf16[48,32,64]{2,1,0:T(8,128)(2,1)S(1)} fusion(bf16[48,48,80]{2,1,0:T(8,128)(2,1)S(1)} %pad_maximum_fusion.14, bf16[]{:T(256)} %bitcast.201, bf16[]{:T(256)} %bitcast.200, bf16[]{:T(256)} %bitcast.199, bf16[]{:T(256)} %bitcast.198, bf16[]{:T(256)} %bitcast.197, bf16[]{:T(256)} %bitcast.196, bf16[]{:T(256)} %bitcast.195, bf16[]{:T(256)} %bitcast.194, ...), kind=kOutput, calls=%fused_computation.59 | convolution fusion | flops 33508864 | bytes 565282 | tf_op jit(solution)/shard_map/abc,bw->awc/dot_general | solution.py:77
  630.3 11.6 %convolution_add_fusion.1 = f32[32,32,64]{2,0,1:T(8,128)} fusion(f32[32,32,64]{2,0,1:T(8,128)S(1)} %convolution_add_fusion.2, bf16[48,32,64]{2,1,0:T(8,128)(2,1)S(1)} %fusion.33, bf16[]{:T(256)} %bitcast.201, bf16[]{:T(256)} %bitcast.200, bf16[]{:T(256)} %bitcast.199, bf16[]{:T(256)} %bitcast.198, bf16[]{:T(256)} %bitcast.197, bf16[]{:T(256)} %bitcast.196, ...), kind=kOutput, calls=%fused_computation.56 | convolution fusion | flops 6410752 | bytes 720930 | tf_op jit(solution)/shard_map/abc,aw->wbc/dot_general | solution.py:77
  644.2 11.7 %fusion.32 = bf16[48,32,64]{2,1,0:T(8,128)(2,1)} fusion(bf16[48,48,80]{2,1,0:T(8,128)(2,1)S(1)} %pad_maximum_fusion.14, bf16[]{:T(256)} %bitcast.238, bf16[]{:T(256)} %bitcast.237, bf16[]{:T(256)} %bitcast.236, bf16[]{:T(256)} %bitcast.235, bf16[]{:T(256)} %bitcast.234, bf16[]{:T(256)} %bitcast.233, bf16[]{:T(256)} %bitcast.232, bf16[]{:T(256)} %bitcast.231, ...), kind=kOutput, calls=%fused_computation.58 | convolution fusion | flops 33508864 | bytes 565282 | tf_op jit(solution)/shard_map/abc,bw->awc/dot_general | solution.py:77
  662.2 11.9 %fusion.31 = f32[32,32,64]{2,0,1:T(8,128)S(1)} fusion(f32[32,32,64]{2,0,1:T(8,128)} %copy.204, f32[32,32,64]{2,0,1:T(8,128)} %convolution_add_fusion.1, bf16[48,32,64]{2,1,0:T(8,128)(2,1)} %fusion.32, bf16[]{:T(256)} %bitcast.238, bf16[]{:T(256)} %bitcast.237, bf16[]{:T(256)} %bitcast.236, bf16[]{:T(256)} %bitcast.235, bf16[]{:T(256)} %bitcast.234, ...), kind=kOutput, calls=%fused_computation.55 | convolution fusion | flops 6476288 | bytes 983074 | tf_op jit(solution)/shard_map/abc,aw->wbc/dot_general | solution.py:77
  678.0 13.1 %fusion.17 = f32[64,64,128]{2,0,1:T(8,128)} fusion(bf16[80,64,128]{2,1,0:T(8,128)(2,1)S(1)} %copy-done.5, bf16[]{:T(256)} %bitcast.617, bf16[]{:T(256)} %bitcast.616, bf16[]{:T(256)} %bitcast.615, bf16[]{:T(256)} %bitcast.614, bf16[]{:T(256)} %bitcast.613, bf16[]{:T(256)} %bitcast.612, bf16[]{:T(256)} %bitcast.611, bf16[]{:T(256)} %bitcast.610, ...), kind=kOutput, calls=%fused_computation.40 | convolution fusion | flops 84065280 | bytes 3407906 | tf_op jit(solution)/shard_map/abc,aw->wbc/dot_general | solution.py:77
  693.2 13.0 %fusion.19 = f32[64,64,128]{2,0,1:T(8,128)} fusion(bf16[80,64,128]{2,1,0:T(8,128)(2,1)S(1)} %copy-done.4, bf16[]{:T(256)} %bitcast.599, bf16[]{:T(256)} %bitcast.598, bf16[]{:T(256)} %bitcast.597, bf16[]{:T(256)} %bitcast.596, bf16[]{:T(256)} %bitcast.595, bf16[]{:T(256)} %bitcast.594, bf16[]{:T(256)} %bitcast.593, bf16[]{:T(256)} %bitcast.592, ...), kind=kOutput, calls=%fused_computation.42 | convolution fusion | flops 84065280 | bytes 3407906 | tf_op jit(solution)/shard_map/abc,aw->wbc/dot_general | solution.py:77
  711.4 13.0 %fusion.21 = f32[64,64,128]{2,0,1:T(8,128)} fusion(bf16[80,64,128]{2,1,0:T(8,128)(2,1)S(1)} %fusion.12, bf16[]{:T(256)} %bitcast.581, bf16[]{:T(256)} %bitcast.580, bf16[]{:T(256)} %bitcast.579, bf16[]{:T(256)} %bitcast.578, bf16[]{:T(256)} %bitcast.577, bf16[]{:T(256)} %bitcast.576, bf16[]{:T(256)} %bitcast.575, bf16[]{:T(256)} %bitcast.574, ...), kind=kOutput, calls=%fused_computation.44 | convolution fusion | flops 84065280 | bytes 3407906 | tf_op jit(solution)/shard_map/abc,aw->wbc/dot_general | solution.py:77
  743.4 15.0 %add_convert_fusion.4 = bf16[64,64,128]{2,0,1:T(8,128)(2,1)S(1)} fusion(f32[64,64,128]{2,0,1:T(8,128)S(1)} %copy.214, f32[64,64,128]{2,0,1:T(8,128)} %fusion.17, f32[64,64,128]{2,0,1:T(8,128)} %fusion.21, f32[64,64,128]{2,0,1:T(8,128)} %fusion.19, bf16[80,64,128]{2,1,0:T(8,128)(2,1)S(1)} %copy-done.3, bf16[]{:T(256)} %bitcast.635, bf16[]{:T(256)} %bitcast.634, ...), kind=kOutput, calls=%fused_computation.16 | convolution fusion | flops 86686720 | bytes 10747938 | tf_op jit(solution)/shard_map/abc,aw->wbc/dot_general | solution.py:77
  (348 shorter events, 384.6 us)
Async XLA Ops:
  1.5 66.9 %collective-permute-start.6 = (f32[3,64,128]{2,1,0:T(8,128)}, f32[3,64,128]{2,1,0:T(8,128)S(1)}, u32[]{:S(2)}, u32[]{:S(2)}) collective-permute-start(f32[3,64,128]{2,1,0:T(8,128)} %get-tuple-element.25), channel_id=1, source_target_pairs={{0,8},{8,16},{16,24},{24,0},{1,9},{9,17},{17,25},{25,1},{2,10},{10... | collective-permute-start | bytes 294920 | tf_op jit(solution)/shard_map/ppermute | solution.py:14
  4.6 63.9 %collective-permute-start.7 = (f32[3,64,128]{2,1,0:T(8,128)}, f32[3,64,128]{2,1,0:T(8,128)}, u32[]{:S(2)}, u32[]{:S(2)}) collective-permute-start(f32[3,64,128]{2,1,0:T(8,128)} %get-tuple-element.26), channel_id=1, source_target_pairs={{8,0},{16,8},{24,16},{0,24},{9,1},{17,9},{25,17},{1,25},{10,2},{18... | collective-permute-start | bytes 294920 | tf_op jit(solution)/shard_map/ppermute | solution.py:15
  8.2 62.8 %collective-permute-start.1 = (bf16[8,64,128]{2,1,0:T(8,128)(2,1)}, bf16[8,64,128]{2,1,0:T(8,128)(2,1)}, u32[]{:S(2)}, u32[]{:S(2)}) collective-permute-start(bf16[8,64,128]{2,1,0:T(8,128)(2,1)} %get-tuple-element.21), channel_id=1, source_target_pairs={{8,0},{16,8},{24,16},{0,24},{9,1},{17,9},{25,17},{1,25},{10,2},{18... | collective-permute-start | bytes 393224 | tf_op jit(solution)/shard_map/ppermute | solution.py:15
  10.3 56.2 %collective-permute-start = (bf16[8,64,128]{2,1,0:T(8,128)(2,1)S(1)}, bf16[8,64,128]{2,1,0:T(8,128)(2,1)S(1)}, u32[]{:S(2)}, u32[]{:S(2)}) collective-permute-start(bf16[8,64,128]{2,1,0:T(8,128)(2,1)S(1)} %get-tuple-element.22), channel_id=1, source_target_pairs={{0,8},{8,16},{16,24},{24,0},{1,9},{9,17},{17,25},{25,1},{2,10},{10... | collective-permute-start | bytes 393224 | tf_op jit(solution)/shard_map/ppermute | solution.py:14
  72.8 16.0 %collective-permute-start.2 = (bf16[80,8,128]{2,1,0:T(8,128)(2,1)}, bf16[80,8,128]{2,1,0:T(8,128)(2,1)}, u32[]{:S(2)}, u32[]{:S(2)}) collective-permute-start(bf16[80,8,128]{2,1,0:T(8,128)(2,1)} %get-tuple-element.17), channel_id=1, source_target_pairs={{0,2},{2,4},{4,6},{6,0},{1,3},{3,5},{5,7},{7,1},{8,10},{10,12},{12... | collective-permute-start | bytes 491528 | tf_op jit(solution)/shard_map/ppermute | solution.py:14
  72.9 15.9 %collective-permute-start.3 = (bf16[80,8,128]{2,1,0:T(8,128)(2,1)}, bf16[80,8,128]{2,1,0:T(8,128)(2,1)}, u32[]{:S(2)}, u32[]{:S(2)}) collective-permute-start(bf16[80,8,128]{2,1,0:T(8,128)(2,1)} %get-tuple-element.18), channel_id=1, source_target_pairs={{2,0},{4,2},{6,4},{0,6},{3,1},{5,3},{7,5},{1,7},{10,8},{12,10},{14... | collective-permute-start | bytes 491528 | tf_op jit(solution)/shard_map/ppermute | solution.py:15
  86.8 11.4 %collective-permute-start.11 = (f32[70,70,3]{1,0,2:T(8,128)}, f32[70,70,3]{1,0,2:T(8,128)}, u32[]{:S(2)}, u32[]{:S(2)}) collective-permute-start(f32[70,70,3]{1,0,2:T(8,128)} %copy.165), channel_id=1, source_target_pairs={{1,0},{0,1},{3,2},{2,3},{5,4},{4,5},{7,6},{6,7},{9,8},{8,9},{11,10... | collective-permute-start | bytes 176408 | tf_op jit(solution)/shard_map/ppermute | solution.py:15
  181.9 12.0 %collective-permute-start.18 = (f32[3,32,64]{2,1,0:T(8,128)S(1)}, f32[3,32,64]{2,1,0:T(8,128)S(1)}, u32[]{:S(2)}, u32[]{:S(2)}) collective-permute-start(f32[3,32,64]{2,1,0:T(8,128)S(1)} %get-tuple-element.45), channel_id=1, source_target_pairs={{0,8},{8,16},{16,24},{24,0},{1,9},{9,17},{17,25},{25,1},{2,10},{10... | collective-permute-start | bytes 73736 | tf_op jit(solution)/shard_map/ppermute | solution.py:14
  182.0 11.9 %collective-permute-start.19 = (f32[3,32,64]{2,1,0:T(8,128)S(1)}, f32[3,32,64]{2,1,0:T(8,128)S(1)}, u32[]{:S(2)}, u32[]{:S(2)}) collective-permute-start(f32[3,32,64]{2,1,0:T(8,128)S(1)} %get-tuple-element.46), channel_id=1, source_target_pairs={{8,0},{16,8},{24,16},{0,24},{9,1},{17,9},{25,17},{1,25},{10,2},{18... | collective-permute-start | bytes 73736 | tf_op jit(solution)/shard_map/ppermute | solution.py:15
  191.9 71.2 %collective-permute-start.5 = (bf16[80,80,8]{1,2,0:T(8,128)(2,1)}, bf16[80,80,8]{1,2,0:T(8,128)(2,1)}, u32[]{:S(2)}, u32[]{:S(2)}) collective-permute-start(bf16[80,80,8]{1,2,0:T(8,128)(2,1)} %copy.148), channel_id=1, source_target_pairs={{1,0},{0,1},{3,2},{2,3},{5,4},{4,5},{7,6},{6,7},{9,8},{8,9},{11,10... | collective-permute-start | bytes 307208 | tf_op jit(solution)/shard_map/ppermute | solution.py:15
  193.4 65.6 %collective-permute-start.4 = (bf16[80,80,8]{1,2,0:T(8,128)(2,1)}, bf16[80,80,8]{1,2,0:T(8,128)(2,1)}, u32[]{:S(2)}, u32[]{:S(2)}) collective-permute-start(bf16[80,80,8]{1,2,0:T(8,128)(2,1)} %copy.147), channel_id=1, source_target_pairs={{0,1},{1,0},{2,3},{3,2},{4,5},{5,4},{6,7},{7,6},{8,9},{9,8},{10,11... | collective-permute-start | bytes 307208 | tf_op jit(solution)/shard_map/ppermute | solution.py:14
  203.6 23.6 %collective-permute-start.14 = (bf16[48,8,64]{2,1,0:T(8,128)(2,1)S(1)}, bf16[48,8,64]{2,1,0:T(8,128)(2,1)S(1)}, u32[]{:S(2)}, u32[]{:S(2)}) collective-permute-start(bf16[48,8,64]{2,1,0:T(8,128)(2,1)S(1)} %get-tuple-element.49), channel_id=1, source_target_pairs={{0,2},{2,4},{4,6},{6,0},{1,3},{3,5},{5,7},{7,1},{8,10},{10,12},{12... | collective-permute-start | bytes 147464 | tf_op jit(solution)/shard_map/ppermute | solution.py:14
  229.2 26.7 %collective-permute-start.26 = (bf16[32,8,32]{2,1,0:T(8,128)(2,1)S(1)}, bf16[32,8,32]{2,1,0:T(8,128)(2,1)S(1)}, u32[]{:S(2)}, u32[]{:S(2)}) collective-permute-start(bf16[32,8,32]{2,1,0:T(8,128)(2,1)S(1)} %get-tuple-element.71), channel_id=1, source_target_pairs={{0,2},{2,4},{4,6},{6,0},{1,3},{3,5},{5,7},{7,1},{8,10},{10,12},{12... | collective-permute-start | bytes 49160 | tf_op jit(solution)/shard_map/ppermute | solution.py:14
  232.3 13.7 %collective-permute-start.35 = (f32[22,22,3]{2,1,0:T(8,128)S(1)}, f32[22,22,3]{2,1,0:T(8,128)S(1)}, u32[]{:S(2)}, u32[]{:S(2)}) collective-permute-start(f32[22,22,3]{2,1,0:T(8,128)S(1)} %get-tuple-element.54), channel_id=1, source_target_pairs={{1,0},{0,1},{3,2},{2,3},{5,4},{4,5},{7,6},{6,7},{9,8},{8,9},{11,10... | collective-permute-start | bytes 17432 | tf_op jit(solution)/shard_map/ppermute | solution.py:15
  240.6 17.1 %collective-permute-start.27 = (bf16[32,8,32]{2,1,0:T(8,128)(2,1)S(1)}, bf16[32,8,32]{2,1,0:T(8,128)(2,1)S(1)}, u32[]{:S(2)}, u32[]{:S(2)}) collective-permute-start(bf16[32,8,32]{2,1,0:T(8,128)(2,1)S(1)} %get-tuple-element.72), channel_id=1, source_target_pairs={{2,0},{4,2},{6,4},{0,6},{3,1},{5,3},{7,5},{1,7},{10,8},{12,10},{14... | collective-permute-start | bytes 49160 | tf_op jit(solution)/shard_map/ppermute | solution.py:15
  246.0 167.7 %collective-permute-start.17 = (bf16[48,48,8]{1,2,0:T(8,128)(2,1)}, bf16[48,48,8]{1,2,0:T(8,128)(2,1)}, u32[]{:S(2)}, u32[]{:S(2)}) collective-permute-start(bf16[48,48,8]{1,2,0:T(8,128)(2,1)} %copy.169), channel_id=1, source_target_pairs={{1,0},{0,1},{3,2},{2,3},{5,4},{4,5},{7,6},{6,7},{9,8},{8,9},{11,10... | collective-permute-start | bytes 110600 | tf_op jit(solution)/shard_map/ppermute | solution.py:15
  250.9 211.7 %all-to-all-start = ((bf16[32,2,512]{2,1,0:T(2,128)(2,1)}), bf16[32,2,512]{2,1,0:T(2,128)(2,1)}, u32[]{:S(2)}, u32[]{:S(2)}) async-start(bf16[32,2,512]{2,1,0:T(2,128)(2,1)} %reshape.1488), calls=%async_computation | async-start | bytes 131072 | tf_op jit(solution)/shard_map/all_to_all | solution.py:139
  255.9 156.6 %collective-permute-start.16 = (bf16[48,48,8]{1,2,0:T(8,128)(2,1)}, bf16[48,48,8]{1,2,0:T(8,128)(2,1)}, u32[]{:S(2)}, u32[]{:S(2)}) collective-permute-start(bf16[48,48,8]{1,2,0:T(8,128)(2,1)} %copy.168), channel_id=1, source_target_pairs={{0,1},{1,0},{2,3},{3,2},{4,5},{5,4},{6,7},{7,6},{8,9},{9,8},{10,11... | collective-permute-start | bytes 110600 | tf_op jit(solution)/shard_map/ppermute | solution.py:14
  258.7 74.7 %collective-permute-start.28 = (bf16[32,32,8]{2,1,0:T(8,128)(2,1)}, bf16[32,32,8]{2,1,0:T(8,128)(2,1)}, u32[]{:S(2)}, u32[]{:S(2)}) collective-permute-start(bf16[32,32,8]{2,1,0:T(8,128)(2,1)} %get-tuple-element.57), channel_id=1, source_target_pairs={{0,1},{1,0},{2,3},{3,2},{4,5},{5,4},{6,7},{7,6},{8,9},{9,8},{10,11... | collective-permute-start | bytes 49160 | tf_op jit(solution)/shard_map/ppermute | solution.py:14
  259.0 74.4 %collective-permute-start.29 = (bf16[32,32,8]{2,1,0:T(8,128)(2,1)}, bf16[32,32,8]{2,1,0:T(8,128)(2,1)}, u32[]{:S(2)}, u32[]{:S(2)}) collective-permute-start(bf16[32,32,8]{2,1,0:T(8,128)(2,1)} %get-tuple-element.58), channel_id=1, source_target_pairs={{1,0},{0,1},{3,2},{2,3},{5,4},{4,5},{7,6},{6,7},{9,8},{8,9},{11,10... | collective-permute-start | bytes 49160 | tf_op jit(solution)/shard_map/ppermute | solution.py:15
  613.2 15.0 %collective-permute-start.36 = (f32[2,16,32]{2,0,1:T(2,128)S(1)}, f32[2,16,32]{2,0,1:T(2,128)S(1)}, u32[]{:S(2)}, u32[]{:S(2)}) collective-permute-start(f32[2,16,32]{2,0,1:T(2,128)S(1)} %get-tuple-element.69), channel_id=1, source_target_pairs={{0,8},{8,16},{16,24},{24,0},{1,9},{9,17},{17,25},{25,1},{2,10},{10... | collective-permute-start | bytes 12296 | tf_op jit(solution)/shard_map/ppermute | solution.py:14
  614.7 13.5 %collective-permute-start.37 = (f32[2,16,32]{2,0,1:T(2,128)S(1)}, f32[2,16,32]{2,0,1:T(2,128)S(1)}, u32[]{:S(2)}, u32[]{:S(2)}) collective-permute-start(f32[2,16,32]{2,0,1:T(2,128)S(1)} %get-tuple-element.70), channel_id=1, source_target_pairs={{8,0},{16,8},{24,16},{0,24},{9,1},{17,9},{25,17},{1,25},{10,2},{18... | collective-permute-start | bytes 12296 | tf_op jit(solution)/shard_map/ppermute | solution.py:15
  628.3 13.6 %collective-permute-start.38 = (f32[20,2,32]{2,0,1:T(8,128)S(1)}, f32[20,2,32]{2,0,1:T(8,128)S(1)}, u32[]{:S(2)}, u32[]{:S(2)}) collective-permute-start(f32[20,2,32]{2,0,1:T(8,128)S(1)} %get-tuple-element.67), channel_id=1, source_target_pairs={{0,2},{2,4},{4,6},{6,0},{1,3},{3,5},{5,7},{7,1},{8,10},{10,12},{12... | collective-permute-start | bytes 15368 | tf_op jit(solution)/shard_map/ppermute | solution.py:14
  628.6 13.4 %collective-permute-start.39 = (f32[20,2,32]{2,0,1:T(8,128)S(1)}, f32[20,2,32]{2,0,1:T(8,128)S(1)}, u32[]{:S(2)}, u32[]{:S(2)}) collective-permute-start(f32[20,2,32]{2,0,1:T(8,128)S(1)} %get-tuple-element.68), channel_id=1, source_target_pairs={{2,0},{4,2},{6,4},{0,6},{3,1},{5,3},{7,5},{1,7},{10,8},{12,10},{14... | collective-permute-start | bytes 15368 | tf_op jit(solution)/shard_map/ppermute | solution.py:15
  642.1 13.8 %collective-permute-start.40 = (f32[20,20,2]{2,0,1:T(8,128)S(1)}, f32[20,20,2]{2,0,1:T(8,128)S(1)}, u32[]{:S(2)}, u32[]{:S(2)}) collective-permute-start(f32[20,20,2]{2,0,1:T(8,128)S(1)} %get-tuple-element.63), channel_id=1, source_target_pairs={{0,1},{1,0},{2,3},{3,2},{4,5},{5,4},{6,7},{7,6},{8,9},{9,8},{10,11... | collective-permute-start | bytes 9608 | tf_op jit(solution)/shard_map/ppermute | solution.py:14
  642.5 13.4 %collective-permute-start.41 = (f32[20,20,2]{2,0,1:T(8,128)S(1)}, f32[20,20,2]{2,0,1:T(8,128)S(1)}, u32[]{:S(2)}, u32[]{:S(2)}) collective-permute-start(f32[20,20,2]{2,0,1:T(8,128)S(1)} %get-tuple-element.64), channel_id=1, source_target_pairs={{1,0},{0,1},{3,2},{2,3},{5,4},{4,5},{7,6},{6,7},{9,8},{8,9},{11,10... | collective-permute-start | bytes 9608 | tf_op jit(solution)/shard_map/ppermute | solution.py:15
  674.2 17.0 %collective-permute-start.42 = (f32[2,32,64]{2,0,1:T(2,128)S(1)}, f32[2,32,64]{2,0,1:T(2,128)S(1)}, u32[]{:S(2)}, u32[]{:S(2)}) collective-permute-start(f32[2,32,64]{2,0,1:T(2,128)S(1)} %get-tuple-element.41), channel_id=1, source_target_pairs={{0,8},{8,16},{16,24},{24,0},{1,9},{9,17},{17,25},{25,1},{2,10},{10... | collective-permute-start | bytes 49160 | tf_op jit(solution)/shard_map/ppermute | solution.py:14
  674.2 16.9 %collective-permute-start.43 = (f32[2,32,64]{2,0,1:T(2,128)S(1)}, f32[2,32,64]{2,0,1:T(2,128)S(1)}, u32[]{:S(2)}, u32[]{:S(2)}) collective-permute-start(f32[2,32,64]{2,0,1:T(2,128)S(1)} %get-tuple-element.42), channel_id=1, source_target_pairs={{8,0},{16,8},{24,16},{0,24},{9,1},{17,9},{25,17},{1,25},{10,2},{18... | collective-permute-start | bytes 49160 | tf_op jit(solution)/shard_map/ppermute | solution.py:15
  691.2 15.1 %collective-permute-start.44 = (f32[36,2,64]{2,0,1:T(8,128)S(1)}, f32[36,2,64]{2,0,1:T(8,128)S(1)}, u32[]{:S(2)}, u32[]{:S(2)}) collective-permute-start(f32[36,2,64]{2,0,1:T(8,128)S(1)} %get-tuple-element.37), channel_id=1, source_target_pairs={{0,2},{2,4},{4,6},{6,0},{1,3},{3,5},{5,7},{7,1},{8,10},{10,12},{12... | collective-permute-start | bytes 55304 | tf_op jit(solution)/shard_map/ppermute | solution.py:14
  691.3 15.0 %collective-permute-start.45 = (f32[36,2,64]{2,0,1:T(8,128)S(1)}, f32[36,2,64]{2,0,1:T(8,128)S(1)}, u32[]{:S(2)}, u32[]{:S(2)}) collective-permute-start(f32[36,2,64]{2,0,1:T(8,128)S(1)} %get-tuple-element.38), channel_id=1, source_target_pairs={{2,0},{4,2},{6,4},{0,6},{3,1},{5,3},{7,5},{1,7},{10,8},{12,10},{14... | collective-permute-start | bytes 55304 | tf_op jit(solution)/shard_map/ppermute | solution.py:15
  709.3 15.5 %collective-permute-start.47 = (f32[36,36,2]{1,2,0:T(2,128)S(1)}, f32[36,36,2]{1,2,0:T(2,128)S(1)}, u32[]{:S(2)}, u32[]{:S(2)}) collective-permute-start(f32[36,36,2]{1,2,0:T(2,128)S(1)} %copy.206), channel_id=1, source_target_pairs={{1,0},{0,1},{3,2},{2,3},{5,4},{4,5},{7,6},{6,7},{9,8},{8,9},{11,10... | collective-permute-start | bytes 31112 | tf_op jit(solution)/shard_map/ppermute | solution.py:15
  709.7 14.7 %collective-permute-start.46 = (f32[36,36,2]{1,2,0:T(2,128)S(1)}, f32[36,36,2]{1,2,0:T(2,128)S(1)}, u32[]{:S(2)}, u32[]{:S(2)}) collective-permute-start(f32[36,36,2]{1,2,0:T(2,128)S(1)} %copy.205), channel_id=1, source_target_pairs={{0,1},{1,0},{2,3},{3,2},{4,5},{5,4},{6,7},{7,6},{8,9},{9,8},{10,11... | collective-permute-start | bytes 31112 | tf_op jit(solution)/shard_map/ppermute | solution.py:14
  (50 other events, 857.2 us)
